TPU v7x, 256 devices: a whole 4x4x8 slice. The times are simulated.
256 devices in a mesh: rows: 32 (over x, z), grp: 8 (over y, core).
Axes of the slice: x: 4, y: 4, z: 8, core: 2. Of those that a mesh axis runs over, the one named last changes fastest.
Arguments:
- embeddings: bfloat16 [131072, 1024], P(('rows', 'grp')), may hold values from -6 to 6
- coarse_ids: int32 [131072], P(('rows', 'grp')), may hold values from 0 to 2047, as said below
- fine_ids: int32 [131072], P(('rows', 'grp')), may hold values from 0 to 63, as said below
- coarse_old: float32 [2048, 1024], P(('rows', 'grp')), may hold values from -6 to 6
- fine_old: float32 [2048, 64, 1024], P('rows', 'grp'), may hold values from -6 to 6
Outputs:
- coarse_new: float32 [2048, 1024], P(('rows', 'grp'))
- fine_new: float32 [2048, 64, 1024], P('rows', 'grp')
- distances: float32 [131072], P(('rows', 'grp'))
Inputs may be any that keep to these rules, and one draw needn't show every extreme that they name: Among the 512 rows of one device, at most 4 have the same pair (coarse_ids // 64, fine_ids // 8), and in every such block some pair has exactly 4. `fine_ids`: within each coarse cluster's fine centroids.
All inputs are finite; a program needn't handle non-finite values.
Results may differ from a plain program's by a relative error of at most 0.0003.
Values may be sent and summed in bfloat16 or wider, within the bound.
No kernel may reach another device: no remote copies, remote signals or barrier semaphores. Data moves between devices by JAX's collectives and lax.ppermute only.
A program may use at most 64 MiB of HBM per device.

v0:
```python
import math

import jax
import jax.numpy as jnp
from jax import lax
from jax.sharding import PartitionSpec as P


def in_blocks(x, dim, devices):
    before, after = (x.shape[:dim], x.shape[dim + 1 :])
    return jnp.moveaxis(x.reshape(*before, devices, -1, *after), dim, 0)


def in_order(tiles, dim):
    shape = list(tiles.shape[1:])
    shape[dim] *= tiles.shape[0]
    return jnp.moveaxis(tiles, 0, dim).reshape(shape)


def exchange_both(x, axis, axes, splits, concats):
    sizes = [lax.axis_size(a) for a in axes]
    tiles = in_blocks(x, splits[0], sizes[0])
    tiles = jnp.moveaxis(in_blocks(tiles, splits[1] + 1, sizes[1]), 0, 1)
    inside = tiles.shape[2:]
    tiles = tiles.reshape(-1, *inside)
    tiles = lax.all_to_all(tiles, axis, split_axis=0, concat_axis=0, tiled=True)
    tiles = in_order(tiles.reshape(*sizes, *inside), concats[0] + 1)
    return in_order(tiles, concats[1])


def summed_on_arrival(x, axis, dim):
    devices = lax.axis_size(axis)
    tiles = lax.all_to_all(in_blocks(x, dim, devices), axis, 0, 0, tiled=True)
    return jnp.sum(tiles, axis=0)


def side_by_side(arrays, axis, dim, along):
    widths = [math.prod(a.shape[along:]) for a in arrays]
    both = jnp.concatenate(
        [a.reshape(*a.shape[:along], w) for a, w in zip(arrays, widths)], axis=along
    )
    result = summed_on_arrival(both, axis, dim)
    tiles = jnp.split(result, [sum(widths[:k]) for k in range(1, len(widths))], axis=along)
    return tuple(
        (b.reshape(*result.shape[:along], *a.shape[along:]) for a, b in zip(arrays, tiles))
    )


def on_device(embeddings, coarse_ids, fine_ids, coarse_old, fine_old):
    owners = lax.axis_size("rows")
    groups = lax.axis_size("grp")
    dests = owners * groups
    local_rows = embeddings.shape[0]
    width = embeddings.shape[1]
    slot_count = max(2, 2 * local_rows // dests)
    per_owner = fine_old.shape[0]
    per_group = fine_old.shape[1]
    target = coarse_ids // per_owner * groups + fine_ids // per_group
    local_index = coarse_ids % per_owner * per_group + fine_ids % per_group
    dest_table = (target[:, None] == jnp.arange(dests, dtype=jnp.int32)[None, :]).astype(jnp.int32)
    earlier = jnp.cumsum(dest_table, axis=0) - dest_table
    rank_in = jnp.sum(earlier * dest_table, axis=1)
    position = target * slot_count + rank_in
    send_rows = jnp.zeros((dests * slot_count, width), jnp.bfloat16).at[position].set(embeddings)
    send_index = jnp.full((dests * slot_count,), -1, jnp.int32).at[position].set(local_index)
    send_rows = send_rows.reshape(owners, groups, slot_count, width)
    send_index = send_index.reshape(owners, groups, slot_count)
    got_rows, got_index = (
        exchange_both(send_rows, ("rows", "grp"), ("rows", "grp"), (0, 1), (0, 1)),
        exchange_both(send_index, ("rows", "grp"), ("rows", "grp"), (0, 1), (0, 1)),
    )
    flat_rows = got_rows.reshape(-1, width)
    flat_index = got_index.reshape(-1)
    centroid_count = per_owner * per_group
    member = jnp.arange(centroid_count, dtype=jnp.int32)[:, None] == flat_index[None, :]
    fine_sums = jnp.dot(member.astype(jnp.bfloat16), flat_rows, preferred_element_type=jnp.float32)
    fine_counts = jnp.sum(member.astype(jnp.float32), axis=1)
    fine_flat = (fine_old.reshape(centroid_count, width) + fine_sums) / (1.0 + fine_counts)[:, None]
    picked = fine_flat[jnp.maximum(flat_index, 0)]
    diff = flat_rows.astype(jnp.float32) - picked
    row_dist = jnp.where(flat_index >= 0, jnp.mean(diff * diff, axis=1), 0.0)
    returned = exchange_both(
        row_dist.reshape(owners, groups, slot_count),
        ("rows", "grp"),
        ("rows", "grp"),
        (0, 1),
        (0, 1),
    )
    distances = returned.reshape(-1)[position]
    partial_sums = jnp.sum(fine_sums.reshape(per_owner, per_group, width), axis=1)
    partial_counts = jnp.sum(fine_counts.reshape(per_owner, per_group), axis=1)
    coarse_sums, coarse_counts = side_by_side((partial_sums, partial_counts), "grp", 0, 1)
    coarse_new = (coarse_old + coarse_sums) / (1.0 + coarse_counts)[:, None]
    return (coarse_new, fine_flat.reshape(fine_old.shape), distances)


def solution(mesh):
    return jax.shard_map(
        on_device,
        mesh=mesh,
        in_specs=(
            P(("rows", "grp"), None),
            P(("rows", "grp")),
            P(("rows", "grp")),
            P(("rows", "grp"), None),
            P("rows", "grp", None),
        ),
        out_specs=(P(("rows", "grp"), None), P("rows", "grp", None), P(("rows", "grp"))),
        check_vma=False,
    )
```

profile of v0, /device:TPU:1, one launch (start us, length us, event | category | flops | bytes accessed | tf_op | source)
XLA Modules:
  0.0 147.0 jit_solution(4033891404994807491)
XLA Ops:
  0.6 0.7 fusion.15
  1.3 0.1 copy.55
  1.5 0.2 fusion.7
  1.8 0.1 copy.56
  1.9 0.2 fusion.6
  2.1 2.4 %scatter_custom_fusion = s32[1024]{0:T(1024)S(1)} fusion(s32[512]{0:T(512)S(1)} %compare_select_fusion, s32[512]{0:T(512)S(1)} %get-tuple-element.3, s32[]{:T(128)} %constant.58.clone.1), kind=kCustom, calls=%fused_computation.52 | custom fusion | bytes 4100 | tf_op jit(solution)/shard_map/scatter | solution.py:65
  4.6 0.8 reshape_transpose_transpose_reshape_reshape_reshape.7
  5.3 15.6 %all-to-all-start = ((s32[256,1,1,4]{3,2,1,0:T(1,128)}), s32[256,1,1,4]{3,2,1,0:T(1,128)S(1)}, u32[]{:S(2)}, u32[]{:S(2)}) async-start(s32[256,1,1,4]{3,2,1,0:T(1,128)} %bitcast.4), calls=%async_computation | async-start | bytes 262144 | tf_op jit(solution)/shard_map/all_to_all | solution.py:26
  21.0 3.9 %scatter_custom_fusion.1 = bf16[1024,1024]{1,0:T(8,128)(2,1)S(1)} fusion(s32[512]{0:T(512)S(1)} %compare_select_fusion, bf16[512,1024]{1,0:T(8,128)(2,1)} %param.5, bf16[]{:T(256)} %constant.69.clone.1), kind=kCustom, calls=%fused_computation.11 | custom fusion | bytes 2097664 | tf_op jit(solution)/shard_map/scatter | solution.py:64
  24.9 2.2 %reshape_transpose_transpose_reshape_reshape_reshape.8 = bf16[256,1,1,4,1024]{4,3,0,2,1:T(4,128)(2,1)} reshape(bf16[1024,1024]{1,0:T(8,128)(2,1)S(1)} %scatter_custom_fusion.1) | data formatting | bytes 4194304 | tf_op jit(solution)/shard_map/reshape;transpose;transpose;reshape;reshape;reshape | solution.py:25
  27.1 6.7 %all-to-all-done = s32[256,1,1,4]{3,2,1,0:T(1,128)S(1)} async-done(((s32[256,1,1,4]{3,2,1,0:T(1,128)}), s32[256,1,1,4]{3,2,1,0:T(1,128)S(1)}, u32[]{:S(2)}, u32[]{:S(2)}) %all-to-all-start) | async-done | bytes 4128 | tf_op jit(solution)/shard_map/all_to_all | solution.py:26
  33.9 7.0 %all-to-all-start.1 = ((bf16[256,1,1,4,1024]{4,3,2,1,0:T(4,128)(2,1)}), bf16[256,1,1,4,1024]{4,3,2,1,0:T(4,128)(2,1)S(1)}, u32[]{:S(2)}, u32[]{:S(2)}) async-start(bf16[256,1,1,4,1024]{4,3,2,1,0:T(4,128)(2,1)} %bitcast.67), calls=%async_computation.1 | async-start | bytes 4194304 | tf_op jit(solution)/shard_map/all_to_all | solution.py:26
  40.8 0.1 eq.49
  41.0 0.3 convert_reduce_fusion
  41.2 0.1 reshape.112
  41.3 0.1 reduce_sum.57
  41.5 0.1 concatenate.11
  41.6 0.1 copy.64
  41.8 0.1 reshape.119
  41.9 52.3 %all-to-all-done.1 = bf16[256,1,1,4,1024]{4,3,2,1,0:T(4,128)(2,1)S(1)} async-done(((bf16[256,1,1,4,1024]{4,3,2,1,0:T(4,128)(2,1)}), bf16[256,1,1,4,1024]{4,3,2,1,0:T(4,128)(2,1)S(1)}, u32[]{:S(2)}, u32[]{:S(2)}) %all-to-all-start.1) | async-done | bytes 2097184 | tf_op jit(solution)/shard_map/all_to_all | solution.py:26
  94.2 0.0 copy-start.1
  94.2 2.2 %reshape_reshape.7 = bf16[1024,1024]{1,0:T(8,128)(2,1)} reshape(bf16[32,8,1,4,1024]{4,3,1,0,2:T(4,128)(2,1)S(1)} %bitcast.65) | data formatting | bytes 4194304 | tf_op jit(solution)/shard_map/reshape;reshape | solution.py:72
  96.4 0.0 copy-done.1
  96.4 0.0 copy-start.2
  96.4 3.3 %bitcast_reduce_fusion = (f32[64,1024]{1,0:T(8,128)S(1)}, f32[512,1024]{1,0:T(8,128)S(1)}) fusion(bf16[1024,1024]{1,0:T(8,128)(2,1)} %reshape_reshape.7, s32[1024]{0:T(1024)S(1)} %eq.49), kind=kOutput, calls=%fused_computation.7 | convolution fusion | flops 1074724864 | bytes 4460544 | tf_op jit(solution)/shard_map/dot_general | solution.py:76
  99.7 0.0 copy-done.2
  99.7 0.5 fusion
  100.2 0.0 copy-start
  100.2 5.4 %gather_fusion = f32[1024,1024]{1,0:T(8,128)} fusion(f32[512,1024]{1,0:T(8,128)S(1)} %fusion, s32[1024]{0:T(1024)S(1)} %broadcast_clamp_fusion), kind=kCustom, calls=%fused_computation | custom fusion | bytes 8392704 | tf_op jit(solution)/shard_map/gather | solution.py:79
  105.6 0.0 copy-done
  105.6 5.2 %gather.9 = f32[32,8,1,4,1024]{4,3,1,0,2:T(4,128)} reshape(f32[1024,1024]{1,0:T(8,128)} %gather_fusion) | data formatting | bytes 8388608 | tf_op jit(solution)/shard_map/gather | solution.py:79
  110.8 4.3 %multiply_reduce_fusion = f32[32,8,4]{2,1,0:T(8,128)S(1)} fusion(f32[32,8,1,4,1024]{4,3,1,0,2:T(4,128)} %gather.9, bf16[32,8,1,4,1024]{4,3,1,0,2:T(4,128)(2,1)} %bitcast.66), kind=kLoop, calls=%fused_computation.4 | loop fusion | flops 4193280 | bytes 6295552 | tf_op jit(solution)/shard_map/reduce_sum | solution.py:81
  115.1 0.1 copy.61
  115.3 0.1 copy.62
  115.4 0.1 div.63
  115.5 0.0 copy-start.3
  115.5 0.8 copy.63
  116.3 6.4 %all-to-all-start.3 = ((f32[256,1,1,4]{3,2,1,0:T(1,128)}), f32[256,1,1,4]{3,2,1,0:T(1,128)S(1)}, u32[]{:S(2)}, u32[]{:S(2)}) async-start(f32[256,1,1,4]{3,2,1,0:T(1,128)} %copy.63), calls=%async_computation.3 | async-start | bytes 262144 | tf_op jit(solution)/shard_map/all_to_all | solution.py:26
  122.7 0.7 pad_maximum_fusion
  123.4 12.1 %all-to-all-done.3 = f32[256,1,1,4]{3,2,1,0:T(1,128)S(1)} async-done(((f32[256,1,1,4]{3,2,1,0:T(1,128)}), f32[256,1,1,4]{3,2,1,0:T(1,128)S(1)}, u32[]{:S(2)}, u32[]{:S(2)}) %all-to-all-start.3) | async-done | bytes 4128 | tf_op jit(solution)/shard_map/all_to_all | solution.py:26
  135.6 3.8 %all-to-all-start.2 = ((f32[8,8,1025]{2,1,0:T(8,128)}), f32[8,8,1025]{2,1,0:T(8,128)S(1)}, u32[]{:S(2)}, u32[]{:S(2)}) async-start(f32[8,8,1025]{2,1,0:T(8,128)} %pad_maximum_fusion), calls=%async_computation.2 | async-start | bytes 589824 | tf_op jit(solution)/shard_map/all_to_all | solution.py:33
  139.4 0.1 reshape_reshape.8
  139.5 3.4 %gather_fusion.1 = f32[512]{0:T(512)} fusion(f32[1024]{0:T(1024)S(1)} %reshape_reshape.8, s32[1024]{0:T(1024)S(1)} %pad_clamp_fusion), kind=kCustom, calls=%fused_computation.1 | custom fusion | bytes 6144 | tf_op jit(solution)/shard_map/gather | solution.py:89
  143.0 3.3 %all-to-all-done.2 = f32[8,8,1025]{2,1,0:T(8,128)S(1)} async-done(((f32[8,8,1025]{2,1,0:T(8,128)}), f32[8,8,1025]{2,1,0:T(8,128)S(1)}, u32[]{:S(2)}, u32[]{:S(2)}) %all-to-all-start.2) | async-done | bytes 262432 | tf_op jit(solution)/shard_map/all_to_all | solution.py:33
  146.2 0.1 fusion.11
  146.3 0.0 copy-done.3
  146.4 0.7 fusion.10
  (14 shorter events, 0.2 us)
Async XLA Ops:
  5.3 28.5 %all-to-all-start = ((s32[256,1,1,4]{3,2,1,0:T(1,128)}), s32[256,1,1,4]{3,2,1,0:T(1,128)S(1)}, u32[]{:S(2)}, u32[]{:S(2)}) async-start(s32[256,1,1,4]{3,2,1,0:T(1,128)} %bitcast.4), calls=%async_computation | async-start | bytes 262144 | tf_op jit(solution)/shard_map/all_to_all | solution.py:26
  33.9 60.3 %all-to-all-start.1 = ((bf16[256,1,1,4,1024]{4,3,2,1,0:T(4,128)(2,1)}), bf16[256,1,1,4,1024]{4,3,2,1,0:T(4,128)(2,1)S(1)}, u32[]{:S(2)}, u32[]{:S(2)}) async-start(bf16[256,1,1,4,1024]{4,3,2,1,0:T(4,128)(2,1)} %bitcast.67), calls=%async_computation.1 | async-start | bytes 4194304 | tf_op jit(solution)/shard_map/all_to_all | solution.py:26
  94.2 2.3 %copy-start.1 = (bf16[256,1,1,4,1024]{4,3,2,1,0:T(4,128)(2,1)}, bf16[256,1,1,4,1024]{4,3,2,1,0:T(4,128)(2,1)S(1)}, u32[]{:S(2)}) copy-start(bf16[256,1,1,4,1024]{4,3,2,1,0:T(4,128)(2,1)S(1)} %all-to-all-done.1) | copy-start | bytes 6291460
  96.4 3.3 %copy-start.2 = (f32[64,8,1024]{2,1,0:T(8,128)S(1)}, f32[64,8,1024]{2,1,0:T(8,128)}, u32[]{:S(2)}) copy-start(f32[64,8,1024]{2,1,0:T(8,128)} %param.9) | copy-start | bytes 6291460
  100.2 5.5 %copy-start = (f32[512,1024]{1,0:T(8,128)}, f32[512,1024]{1,0:T(8,128)S(1)}, u32[]{:S(2)}) copy-start(f32[512,1024]{1,0:T(8,128)S(1)} %fusion) | copy-start | bytes 6291460
  115.5 30.9 %copy-start.3 = (f32[8,1024]{1,0:T(8,128)S(1)}, f32[8,1024]{1,0:T(8,128)}, u32[]{:S(2)}) copy-start(f32[8,1024]{1,0:T(8,128)} %param.8) | copy-start | bytes 98308
  116.3 19.3 %all-to-all-start.3 = ((f32[256,1,1,4]{3,2,1,0:T(1,128)}), f32[256,1,1,4]{3,2,1,0:T(1,128)S(1)}, u32[]{:S(2)}, u32[]{:S(2)}) async-start(f32[256,1,1,4]{3,2,1,0:T(1,128)} %copy.63), calls=%async_computation.3 | async-start | bytes 262144 | tf_op jit(solution)/shard_map/all_to_all | solution.py:26
  135.6 10.6 %all-to-all-start.2 = ((f32[8,8,1025]{2,1,0:T(8,128)}), f32[8,8,1025]{2,1,0:T(8,128)S(1)}, u32[]{:S(2)}, u32[]{:S(2)}) async-start(f32[8,8,1025]{2,1,0:T(8,128)} %pad_maximum_fusion), calls=%async_computation.2 | async-start | bytes 589824 | tf_op jit(solution)/shard_map/all_to_all | solution.py:33
where the time goes:
time: 148 us; the launch traced here: 147 us
  waiting for transfers between devices  74.4 us (50%)
  starting transfers between devices  32.9 us (22%)
  local copies, waits for them, and re-layouts  27.6 us (19%)
  other arithmetic  8.05 us (5%)
  matrix products  3.28 us (2%)
    all_to_all x3, waiting for transfers between devices, exchange_both(): tiles = lax.all_to_all(tiles, axis, split_axis=0, concat_axis=0, tiled=True)  71.1 us
    all_to_all x3, starting transfers between devices, exchange_both(): tiles = lax.all_to_all(tiles, axis, split_axis=0, concat_axis=0, tiled=True)  29 us
    gather x2, local copies, waits for them, and re-layouts, on_device(): picked = fine_flat[jnp.maximum(flat_index, 0)]  10.6 us
    reduce_sum x1, other arithmetic, on_device(): row_dist = jnp.where(flat_index >= 0, jnp.mean(diff * diff, axis=1), 0.0)  4.32 us
    scatter x1, local copies, waits for them, and re-layouts, on_device(): jnp.zeros((dests * slot_count, width), jnp.bfloat16).at[position]  3.89 us
    all_to_all x1, starting transfers between devices, summed_on_arrival(): tiles = lax.all_to_all(in_blocks(x, dim, devices), axis, 0, 0, tiled=True)  3.84 us
    gather x1, local copies, waits for them, and re-layouts, on_device(): distances = returned.reshape(-1)[position]  3.42 us
    dot_general x1, matrix products, on_device(): jnp.dot(member.astype(jnp.bfloat16), flat_rows, preferred_element_type=jn...  3.28 us
  transfers between devices with their start and end apart: 4, of which 4 were waited for; matrix products, arithmetic and copies ran while one was open for 8% of the time, Pallas kernels for 0%

commit v1 on v0

v1 whole, which is shorter than its diff:
```python
import functools

import jax
import jax.numpy as jnp
from jax import lax
from jax.experimental import pallas as pl
from jax.experimental.pallas import tpu as pltpu
from jax.sharding import PartitionSpec as P


AXES = ("rows", "grp")
SLOTS = 4
LANES = 128


def log2(n):
    assert n & (n - 1) == 0
    return n.bit_length() - 1


def iota(shape, dim):
    return lax.broadcasted_iota(jnp.int32, shape, dim)


def pack_kernel(coarse_ref, fine_ref, emb_ref, msg_ref, pos_ref, hot_ref, wide_ref, *, dests, groups, kc, fg):
    rows, width = emb_ref.shape
    lane_groups = width // LANES
    per_msg = SLOTS * lane_groups + 2
    coarse, fine = coarse_ref[...], fine_ref[...]
    dest = (coarse >> log2(kc)) * groups + (fine >> log2(fg))
    local = ((coarse & (kc - 1)) << log2(fg)) + (fine & (fg - 1))
    down = jnp.transpose(jnp.broadcast_to(dest, (LANES, rows)))
    ranks = []
    for j in range(0, rows, LANES):
        before = iota((rows, LANES), 0) < iota((rows, LANES), 1) + j
        same = (down == dest[:, j : j + LANES]) & before
        ranks.append(jnp.sum(jnp.where(same, 1.0, 0.0), axis=0, keepdims=True))
    rank = jnp.concatenate(ranks, axis=1).astype(jnp.int32)
    pos = rank * dests + dest
    pos_ref[...] = pos
    lane = iota((dests, LANES), 1)
    named = jnp.zeros((dests, LANES), jnp.int32)
    mark = (local + 1).astype(jnp.float32)
    for s in range(SLOTS):
        hit = iota((dests, rows), 0) + s * dests == pos
        hot_ref[s * dests : (s + 1) * dests, :] = jnp.where(hit, 1.0, 0.0).astype(jnp.bfloat16)
        found = jnp.sum(jnp.where(hit, mark, 0.0), axis=1, keepdims=True).astype(jnp.int32)
        named = jnp.where(lane == s, found, named)
    named = named - 1
    wide_ref[pl.ds(SLOTS * lane_groups, dests, stride=per_msg), :] = (named >> log2(fg)).astype(jnp.float32)
    wide_ref[pl.ds(SLOTS * lane_groups + 1, dests, stride=per_msg), :] = (named & (fg - 1)).astype(jnp.float32)
    step = 2 * LANES
    for n in range(width // step):
        got = jnp.dot(hot_ref[...], emb_ref[:, n * step : (n + 1) * step], preferred_element_type=jnp.float32)
        for h in range(2):
            for s in range(SLOTS):
                wide_ref[pl.ds(s * lane_groups + 2 * n + h, dests, stride=per_msg), :] = got[
                    s * dests : (s + 1) * dests, h * LANES : (h + 1) * LANES
                ]
    msg_ref[...] = wide_ref[...].astype(jnp.bfloat16)


def update_kernel(msg_ref, old_ref, new_ref, coarse_ref, x_ref, key_ref, wide_ref, mem_ref, *, dests, kc, fg):
    cells, width = old_ref.shape
    lane_groups = width // LANES
    per_msg = SLOTS * lane_groups + 2
    slots = SLOTS * dests
    wide_ref[...] = msg_ref[...].astype(jnp.float32)
    high = wide_ref[pl.ds(SLOTS * lane_groups, dests, stride=per_msg), :]
    low = wide_ref[pl.ds(SLOTS * lane_groups + 1, dests, stride=per_msg), :]
    key = high * fg + low
    key_ref[...] = key
    across = jnp.transpose(key)
    keys = jnp.concatenate([across[s : s + 1, :] for s in range(SLOTS)], axis=1).astype(jnp.int32)
    for s in range(SLOTS):
        for g in range(lane_groups):
            part = wide_ref[pl.ds(s * lane_groups + g, dests, stride=per_msg), :]
            x_ref[s * dests : (s + 1) * dests, g * LANES : (g + 1) * LANES] = part.astype(jnp.bfloat16)
    member = jnp.where(iota((cells, slots), 0) == keys, 1.0, 0.0)
    mem_ref[:cells, :] = member.astype(jnp.bfloat16)
    counts = jnp.sum(member, axis=1, keepdims=True)
    member = jnp.where(iota((kc, slots), 0) == (keys >> log2(fg)), 1.0, 0.0)
    mem_ref[cells:, :] = member.astype(jnp.bfloat16)
    coarse_counts = jnp.sum(member, axis=1, keepdims=True)
    coarse_ref[:, width:] = jnp.broadcast_to(coarse_counts, (kc, LANES))
    step = 2 * LANES
    for n in range(width // step):
        at = slice(n * step, (n + 1) * step)
        sums = jnp.dot(mem_ref[...], x_ref[:, at], preferred_element_type=jnp.float32)
        new_ref[:, at] = (old_ref[:, at] + sums[:cells]) / (1.0 + counts)
        coarse_ref[:, at] = sums[cells:]


def distance_kernel(x_ref, new_ref, key_ref, dist_ref, hot_ref, acc_ref, *, dests):
    cells, width = new_ref.shape
    key = key_ref[...].astype(jnp.int32)
    for s in range(SLOTS):
        hit = iota((dests, cells), 1) == key[:, s : s + 1]
        hot_ref[s * dests : (s + 1) * dests, :] = jnp.where(hit, 1.0, 0.0).astype(jnp.bfloat16)
    step = 2 * LANES
    for n in range(width // step):
        at = slice(n * step, (n + 1) * step)
        new = new_ref[:, at]
        top = new.astype(jnp.bfloat16)
        rest = new - top.astype(jnp.float32)
        mid = rest.astype(jnp.bfloat16)
        end = (rest - mid.astype(jnp.float32)).astype(jnp.bfloat16)
        hot = hot_ref[...]
        picked = jnp.dot(hot, top, preferred_element_type=jnp.float32)
        picked += jnp.dot(hot, mid, preferred_element_type=jnp.float32)
        picked += jnp.dot(hot, end, preferred_element_type=jnp.float32)
        diff = x_ref[:, at].astype(jnp.float32) - picked
        diff = diff * diff
        both = diff[:, :LANES] + diff[:, LANES:]
        if n == 0:
            acc_ref[...] = both
        else:
            acc_ref[...] += both
    for s in range(SLOTS):
        total = jnp.sum(acc_ref[s * dests : (s + 1) * dests, :], axis=1, keepdims=True)
        dist_ref[:, s : s + 1] = total * (1.0 / width)


def finish_kernel(back_ref, pos_ref, out_ref, *, dests):
    pos = pos_ref[...]
    total = jnp.zeros(pos.shape, jnp.float32)
    for s in range(SLOTS):
        hit = iota((dests, pos.shape[1]), 0) + s * dests == pos
        total += jnp.sum(jnp.where(hit, back_ref[:, s : s + 1], 0.0), axis=0, keepdims=True)
    out_ref[...] = total


def call(kernel, outs, scratch=(), limit=24 << 20):
    return pl.pallas_call(
        kernel,
        out_shape=outs,
        scratch_shapes=list(scratch),
        compiler_params=pltpu.CompilerParams(vmem_limit_bytes=limit),
    )


def on_device(embeddings, coarse_ids, fine_ids, coarse_old, fine_old):
    groups = lax.axis_size("grp")
    dests = lax.axis_size("rows") * groups
    rows, width = embeddings.shape
    kc, fg = fine_old.shape[:2]
    cells, slots = kc * fg, SLOTS * dests
    per_msg = SLOTS * (width // LANES) + 2
    f32, bf16 = jnp.float32, jnp.bfloat16
    shape = jax.ShapeDtypeStruct
    msg, pos = call(
        functools.partial(pack_kernel, dests=dests, groups=groups, kc=kc, fg=fg),
        (shape((dests * per_msg, LANES), bf16), shape((1, rows), jnp.int32)),
        (pltpu.VMEM((slots, rows), bf16), pltpu.VMEM((dests * per_msg, LANES), f32)),
    )(coarse_ids.reshape(1, rows), fine_ids.reshape(1, rows), embeddings)
    msg = lax.all_to_all(msg.reshape(dests, per_msg // 2, 2, LANES), AXES, 0, 0, tiled=True)
    new, coarse, x, key = call(
        functools.partial(update_kernel, dests=dests, kc=kc, fg=fg),
        (
            shape((cells, width), f32),
            shape((kc, width + LANES), f32),
            shape((slots, width), bf16),
            shape((dests, LANES), f32),
        ),
        (pltpu.VMEM((dests * per_msg, LANES), f32), pltpu.VMEM((cells + kc, slots), bf16)),
    )(msg.reshape(dests * per_msg, LANES), fine_old.reshape(cells, width))
    coarse = lax.all_to_all(coarse.reshape(groups, kc // groups, width + LANES), "grp", 0, 0, tiled=True)
    dist = call(
        functools.partial(distance_kernel, dests=dests),
        shape((dests, SLOTS), f32),
        (pltpu.VMEM((slots, cells), bf16), pltpu.VMEM((slots, LANES), f32)),
    )(x, new, key)
    back = lax.all_to_all(dist, AXES, 0, 0, tiled=True)
    coarse = jnp.sum(coarse, axis=0)
    coarse_new = (coarse_old + coarse[:, :width]) / (1.0 + coarse[:, width : width + 1])
    distances = call(
        functools.partial(finish_kernel, dests=dests),
        shape((1, rows), f32),
    )(back, pos)
    return (coarse_new, new.reshape(fine_old.shape), distances.reshape(rows))


def solution(mesh):
    return jax.shard_map(
        on_device,
        mesh=mesh,
        in_specs=(
            P(AXES, None),
            P(AXES),
            P(AXES),
            P(AXES, None),
            P("rows", "grp", None),
        ),
        out_specs=(P(AXES, None), P("rows", "grp", None), P(AXES)),
        check_vma=False,
    )
```

time: 148 us -> 116 us (0.78)
  blocking collectives: 0 us -> 90.7 us
  waiting for transfers between devices: 74.4 us -> 5.89 us
  starting transfers between devices: 32.9 us -> 3.78 us
  local copies, waits for them, and re-layouts: 27.6 us -> 4.18 us
  Pallas kernels: 0 us -> 9.78 us
  other arithmetic: 8.05 us -> 0.83 us
  matrix products: 3.28 us -> 0 us
    all_to_all x0 -> x2, blocking collectives: none -> 90.7 us  [the longest x1 71.6 us: on_device(): lax.all_to_all(msg.reshape(dests, per_msg // 2, 2, LANES), AXES, 0, 0, ti...]
    all_to_all x4 -> x1, waiting for transfers between devices: 74.4 us -> 5.89 us  [on_device(): lax.all_to_all(coarse.reshape(groups, kc // groups, width + LANES), 'grp'...]
    all_to_all x4 -> x1, starting transfers between devices: 32.9 us -> 3.78 us  [on_device(): lax.all_to_all(coarse.reshape(groups, kc // groups, width + LANES), 'grp'...]
    gather x3 -> x0, local copies, waits for them, and re-layouts: 14 us -> none  [the longest x2 10.6 us: on_device(): picked = fine_flat[jnp.maximum(flat_index, 0)]]
    pallas_call x0 -> x4, Pallas kernels: none -> 9.78 us  [the longest x1 3.64 us: on_device(): call(functools.partial(update_kernel, dests=dests, kc=kc, fg=fg), (shape(...]
    scatter x2 -> x0, local copies, waits for them, and re-layouts: 6.34 us -> none  [the longest x1 3.89 us: on_device(): jnp.zeros((dests * slot_count, width), jnp.bfloat16).at[position]]
    another operation x7 -> x0, local copies, waits for them, and re-layouts: 5.45 us -> none  [the longest x2 2.97 us: exchange_both(): tiles = tiles.reshape(-1, *inside)]
    reduce_sum x5 -> x1, other arithmetic: 4.98 us -> 0.02 us  [on_device(): coarse = jnp.sum(coarse, axis=0)]
  transfers between devices with their start and end apart: 4 -> 1, of which waited for: 4 -> 1; matrix products, arithmetic and copies ran while one was open for 8% -> 0% of each run, Pallas kernels for 0% -> 1%
where the time goes in v1:
time: 116 us
  blocking collectives  90.7 us (78%)
  Pallas kernels  9.78 us (8%)
  waiting for transfers between devices  5.89 us (5%)
  local copies, waits for them, and re-layouts  4.18 us (4%)
  starting transfers between devices  3.78 us (3%)
    all_to_all x1, blocking collectives, on_device(): lax.all_to_all(msg.reshape(dests, per_msg // 2, 2, LANES), AXES, 0, 0, ti...  71.6 us
    all_to_all x1, blocking collectives, on_device(): back = lax.all_to_all(dist, AXES, 0, 0, tiled=True)  19 us
    all_to_all x1, waiting for transfers between devices, on_device(): lax.all_to_all(coarse.reshape(groups, kc // groups, width + LANES), 'grp'...  5.89 us
    unnamed x12, local copies, waits for them, and re-layouts  4.18 us
    all_to_all x1, starting transfers between devices, on_device(): lax.all_to_all(coarse.reshape(groups, kc // groups, width + LANES), 'grp'...  3.78 us
    pallas_call x1, Pallas kernels, on_device(): call(functools.partial(update_kernel, dests=dests, kc=kc, fg=fg), (shape(...  3.64 us
    pallas_call x1, Pallas kernels, on_device(): call(functools.partial(distance_kernel, dests=dests), shape((dests, SLOTS...  3.61 us
  transfers between devices with their start and end apart: 1, of which 1 were waited for; matrix products, arithmetic and copies ran while one was open for 0% of the time, Pallas kernels for 1%

profile of v1, /device:TPU:1, one launch (start us, length us, event | category | flops | bytes accessed | tf_op | source)
XLA Modules:
  0.0 115.8 jit_solution(17136283292504291346)
XLA Ops:
  0.6 0.0 copy-start.2
  0.6 1.2 %copy-done.2 = bf16[512,1024]{1,0:T(8,128)(2,1)S(1)} copy-done((bf16[512,1024]{1,0:T(8,128)(2,1)S(1)}, bf16[512,1024]{1,0:T(8,128)(2,1)}, u32[]{:S(2)}) %copy-start.2) | copy-done | bytes 1048600
  1.9 0.0 copy-start.3
  1.9 0.7 copy-done.3
  2.5 0.0 copy-start.4
  2.5 0.7 copy-done.4
  3.2 1.6 %shard_map.76 = (bf16[8704,128]{1,0:T(8,128)(2,1)S(1)}, s32[1,512]{1,0:T(1,128)S(1)}) custom-call(s32[1,512]{1,0:T(1,128)S(1)} %bitcast.18, s32[1,512]{1,0:T(1,128)S(1)} %bitcast.19, bf16[512,1024]{1,0:T(8,128)(2,1)S(1)} %copy-done.2), custom_call_target="tpu_custom_call" | custom-call | tf_op jit(solution)/shard_map/pallas_call | solution.py:151
  4.8 0.0 copy-start
  4.9 71.6 %all_to_all.21 = bf16[256,17,2,128]{3,2,1,0:T(2,128)(2,1)S(1)} all-to-all(bf16[256,17,2,128]{3,2,1,0:T(2,128)(2,1)S(1)} %bitcast.13), channel_id=1, replica_groups=mesh['rows'=32,'grp'=8] {'rows','grp'}, dimensions={0} | all-to-all | bytes 4456448 | tf_op jit(solution)/shard_map/all_to_all | solution.py:156
  76.5 0.0 copy-done
  76.5 3.6 %shard_map.77 = (f32[512,1024]{1,0:T(8,128)}, f32[64,1152]{1,0:T(8,128)}, bf16[1024,1024]{1,0:T(8,128)(2,1)S(1)}, f32[256,128]{1,0:T(8,128)S(1)}) custom-call(bf16[8704,128]{1,0:T(8,128)(2,1)S(1)} %bitcast.12, f32[512,1024]{1,0:T(8,128)S(1)} %bitcast.14), custom_call_target="tpu_custom_call" | custom-call | tf_op jit(solution)/shard_map/pallas_call | solution.py:157
  80.1 0.0 copy-start.1
  80.1 1.6 %copy-done.1 = f32[512,1024]{1,0:T(8,128)S(1)} copy-done((f32[512,1024]{1,0:T(8,128)S(1)}, f32[512,1024]{1,0:T(8,128)}, u32[]{:S(2)}) %copy-start.1) | copy-done | bytes 2097176
  81.7 0.0 copy-start.5
  81.7 3.6 %shard_map.78 = f32[256,4]{1,0:T(8,128)S(1)} custom-call(bf16[1024,1024]{1,0:T(8,128)(2,1)S(1)} %get-tuple-element.12.x_ref, f32[512,1024]{1,0:T(8,128)S(1)} %copy-done.1, f32[256,128]{1,0:T(8,128)S(1)} %get-tuple-element.13.key_ref), custom_call_target="tpu_custom_call" | custom-call | tf_op jit(solution)/shard_map/pallas_call | solution.py:168
  85.3 19.0 %all_to_all.22 = f32[256,1,4]{2,1,0:T(1,128)S(1)} all-to-all(f32[256,1,4]{2,1,0:T(1,128)S(1)} %bitcast.16), channel_id=1, replica_groups=mesh['rows'=32,'grp'=8] {'rows','grp'}, dimensions={0} | all-to-all | bytes 8192 | tf_op jit(solution)/shard_map/all_to_all | solution.py:173
  104.4 3.8 %all-to-all-start.1 = ((f32[8,8,1152]{2,1,0:T(8,128)}), f32[8,8,1152]{2,1,0:T(8,128)S(1)}, u32[]{:S(2)}, u32[]{:S(2)}) async-start(f32[8,8,1152]{2,1,0:T(8,128)} %bitcast.5), calls=%async_computation.1 | async-start | bytes 589824 | tf_op jit(solution)/shard_map/all_to_all | solution.py:167
  108.2 0.9 shard_map.79
  109.1 5.9 %all-to-all-done.1 = f32[8,8,1152]{2,1,0:T(8,128)S(1)} async-done(((f32[8,8,1152]{2,1,0:T(8,128)}), f32[8,8,1152]{2,1,0:T(8,128)S(1)}, u32[]{:S(2)}, u32[]{:S(2)}) %all-to-all-start.1) | async-done | bytes 294944 | tf_op jit(solution)/shard_map/all_to_all | solution.py:167
  115.0 0.1 fusion.1
  115.1 0.0 copy-done.5
  115.1 0.7 fusion
  (1 shorter events, 0.0 us)
Async XLA Ops:
  0.6 1.2 %copy-start.2 = (bf16[512,1024]{1,0:T(8,128)(2,1)S(1)}, bf16[512,1024]{1,0:T(8,128)(2,1)}, u32[]{:S(2)}) copy-start(bf16[512,1024]{1,0:T(8,128)(2,1)} %emb_ref.1) | copy-start | bytes 3145732
  1.9 0.7 copy-start.3
  2.5 0.7 copy-start.4
  4.8 71.6 %copy-start = (f32[64,8,1024]{2,1,0:T(8,128)S(1)}, f32[64,8,1024]{2,1,0:T(8,128)}, u32[]{:S(2)}) copy-start(f32[64,8,1024]{2,1,0:T(8,128)} %param.9) | copy-start | bytes 6291460
  80.1 1.6 %copy-start.1 = (f32[512,1024]{1,0:T(8,128)S(1)}, f32[512,1024]{1,0:T(8,128)}, u32[]{:S(2)}) copy-start(f32[512,1024]{1,0:T(8,128)} %get-tuple-element.11.new_ref) | copy-start | bytes 6291460
  81.7 33.4 %copy-start.5 = (f32[8,1024]{1,0:T(8,128)S(1)}, f32[8,1024]{1,0:T(8,128)}, u32[]{:S(2)}) copy-start(f32[8,1024]{1,0:T(8,128)} %param.8) | copy-start | bytes 98308
  104.4 10.6 %all-to-all-start.1 = ((f32[8,8,1152]{2,1,0:T(8,128)}), f32[8,8,1152]{2,1,0:T(8,128)S(1)}, u32[]{:S(2)}, u32[]{:S(2)}) async-start(f32[8,8,1152]{2,1,0:T(8,128)} %bitcast.5), calls=%async_computation.1 | async-start | bytes 589824 | tf_op jit(solution)/shard_map/all_to_all | solution.py:167

commit v2 on v1

--- a/solution.py
+++ b/solution.py
@@ -22,10 +22,35 @@
     return lax.broadcasted_iota(jnp.int32, shape, dim)
 
 
-def pack_kernel(coarse_ref, fine_ref, emb_ref, msg_ref, pos_ref, hot_ref, wide_ref, *, dests, groups, kc, fg):
+def pack_kernel(
+    coarse_hbm,
+    fine_hbm,
+    emb_hbm,
+    msg_ref,
+    pos_ref,
+    coarse_ref,
+    fine_ref,
+    emb_ref,
+    sems,
+    hot_ref,
+    wide_ref,
+    *,
+    dests,
+    groups,
+    kc,
+    fg,
+):
+    coarse_copy = pltpu.make_async_copy(coarse_hbm, coarse_ref, sems.at[0])
+    fine_copy = pltpu.make_async_copy(fine_hbm, fine_ref, sems.at[1])
+    emb_copy = pltpu.make_async_copy(emb_hbm, emb_ref, sems.at[2])
+    coarse_copy.start()
+    fine_copy.start()
+    emb_copy.start()
     rows, width = emb_ref.shape
     lane_groups = width // LANES
     per_msg = SLOTS * lane_groups + 2
+    coarse_copy.wait()
+    fine_copy.wait()
     coarse, fine = coarse_ref[...], fine_ref[...]
     dest = (coarse >> log2(kc)) * groups + (fine >> log2(fg))
     local = ((coarse & (kc - 1)) << log2(fg)) + (fine & (fg - 1))
@@ -49,6 +74,7 @@
     named = named - 1
     wide_ref[pl.ds(SLOTS * lane_groups, dests, stride=per_msg), :] = (named >> log2(fg)).astype(jnp.float32)
     wide_ref[pl.ds(SLOTS * lane_groups + 1, dests, stride=per_msg), :] = (named & (fg - 1)).astype(jnp.float32)
+    emb_copy.wait()
     step = 2 * LANES
     for n in range(width // step):
         got = jnp.dot(hot_ref[...], emb_ref[:, n * step : (n + 1) * step], preferred_element_type=jnp.float32)
@@ -60,7 +86,7 @@
     msg_ref[...] = wide_ref[...].astype(jnp.bfloat16)
 
 
-def update_kernel(msg_ref, old_ref, new_ref, coarse_ref, x_ref, key_ref, wide_ref, mem_ref, *, dests, kc, fg):
+def update_kernel(msg_ref, old_ref, new_ref, keep_ref, send_ref, x_ref, key_ref, wide_ref, mem_ref, *, dests, groups, kc, fg):
     cells, width = old_ref.shape
     lane_groups = width // LANES
     per_msg = SLOTS * lane_groups + 2
@@ -79,19 +105,27 @@
     member = jnp.where(iota((cells, slots), 0) == keys, 1.0, 0.0)
     mem_ref[:cells, :] = member.astype(jnp.bfloat16)
     counts = jnp.sum(member, axis=1, keepdims=True)
-    member = jnp.where(iota((kc, slots), 0) == (keys >> log2(fg)), 1.0, 0.0)
+    block = iota((kc, slots), 0) >> log2(kc // groups)
+    block = sum(((block >> b) & 1) << (log2(groups) - 1 - b) for b in range(log2(groups)))
+    owned = ((block ^ lax.axis_index("grp")) << log2(kc // groups)) + (iota((kc, slots), 0) & (kc // groups - 1))
+    member = jnp.where(owned == (keys >> log2(fg)), 1.0, 0.0)
     mem_ref[cells:, :] = member.astype(jnp.bfloat16)
     coarse_counts = jnp.sum(member, axis=1, keepdims=True)
-    coarse_ref[:, width:] = jnp.broadcast_to(coarse_counts, (kc, LANES))
+    coarse_counts = jnp.broadcast_to(coarse_counts, (kc, LANES))
+    keep_ref[:, width:] = coarse_counts[: kc // 2]
+    send_ref[:, width:] = coarse_counts[kc // 2 :]
     step = 2 * LANES
     for n in range(width // step):
         at = slice(n * step, (n + 1) * step)
         sums = jnp.dot(mem_ref[...], x_ref[:, at], preferred_element_type=jnp.float32)
         new_ref[:, at] = (old_ref[:, at] + sums[:cells]) / (1.0 + counts)
-        coarse_ref[:, at] = sums[cells:]
-
-
-def distance_kernel(x_ref, new_ref, key_ref, dist_ref, hot_ref, acc_ref, *, dests):
+        keep_ref[:, at] = sums[cells : cells + kc // 2]
+        send_ref[:, at] = sums[cells + kc // 2 :]
+
+
+def distance_kernel(x_ref, new_ref, key_ref, dist_ref, out_hbm, hot_ref, acc_ref, sem, *, dests):
+    out_copy = pltpu.make_async_copy(new_ref, out_hbm, sem)
+    out_copy.start()
     cells, width = new_ref.shape
     key = key_ref[...].astype(jnp.int32)
     for s in range(SLOTS):
@@ -119,6 +153,7 @@
     for s in range(SLOTS):
         total = jnp.sum(acc_ref[s * dests : (s + 1) * dests, :], axis=1, keepdims=True)
         dist_ref[:, s : s + 1] = total * (1.0 / width)
+    out_copy.wait()
 
 
 def finish_kernel(back_ref, pos_ref, out_ref, *, dests):
@@ -130,10 +165,11 @@
     out_ref[...] = total
 
 
-def call(kernel, outs, scratch=(), limit=24 << 20):
+def call(kernel, outs, scratch=(), limit=24 << 20, **specs):
     return pl.pallas_call(
         kernel,
         out_shape=outs,
+        **specs,
         scratch_shapes=list(scratch),
         compiler_params=pltpu.CompilerParams(vmem_limit_bytes=limit),
     )
@@ -148,30 +184,45 @@
     per_msg = SLOTS * (width // LANES) + 2
     f32, bf16 = jnp.float32, jnp.bfloat16
     shape = jax.ShapeDtypeStruct
+    ids = coarse_ids.reshape(1, rows), fine_ids.reshape(1, rows)
     msg, pos = call(
         functools.partial(pack_kernel, dests=dests, groups=groups, kc=kc, fg=fg),
         (shape((dests * per_msg, LANES), bf16), shape((1, rows), jnp.int32)),
-        (pltpu.VMEM((slots, rows), bf16), pltpu.VMEM((dests * per_msg, LANES), f32)),
-    )(coarse_ids.reshape(1, rows), fine_ids.reshape(1, rows), embeddings)
+        (
+            pltpu.VMEM((1, rows), jnp.int32),
+            pltpu.VMEM((1, rows), jnp.int32),
+            pltpu.VMEM((rows, width), bf16),
+            pltpu.SemaphoreType.DMA((3,)),
+            pltpu.VMEM((slots, rows), bf16),
+            pltpu.VMEM((dests * per_msg, LANES), f32),
+        ),
+        in_specs=[pl.BlockSpec(memory_space=pltpu.HBM)] * 3,
+    )(*(pltpu.with_memory_space_constraint(a, pltpu.HBM) for a in (ids[0], ids[1], embeddings)))
     msg = lax.all_to_all(msg.reshape(dests, per_msg // 2, 2, LANES), AXES, 0, 0, tiled=True)
-    new, coarse, x, key = call(
-        functools.partial(update_kernel, dests=dests, kc=kc, fg=fg),
+    new, coarse, away, x, key = call(
+        functools.partial(update_kernel, dests=dests, groups=groups, kc=kc, fg=fg),
         (
             shape((cells, width), f32),
-            shape((kc, width + LANES), f32),
+            shape((kc // 2, width + LANES), f32),
+            shape((kc // 2, width + LANES), f32),
             shape((slots, width), bf16),
             shape((dests, LANES), f32),
         ),
         (pltpu.VMEM((dests * per_msg, LANES), f32), pltpu.VMEM((cells + kc, slots), bf16)),
     )(msg.reshape(dests * per_msg, LANES), fine_old.reshape(cells, width))
-    coarse = lax.all_to_all(coarse.reshape(groups, kc // groups, width + LANES), "grp", 0, 0, tiled=True)
-    dist = call(
+    dist, new = call(
         functools.partial(distance_kernel, dests=dests),
-        shape((dests, SLOTS), f32),
-        (pltpu.VMEM((slots, cells), bf16), pltpu.VMEM((slots, LANES), f32)),
+        (shape((dests, SLOTS), f32), shape((cells, width), f32)),
+        (pltpu.VMEM((slots, cells), bf16), pltpu.VMEM((slots, LANES), f32), pltpu.SemaphoreType.DMA(())),
+        out_specs=(pl.BlockSpec(memory_space=pltpu.VMEM), pl.BlockSpec(memory_space=pltpu.HBM)),
     )(x, new, key)
     back = lax.all_to_all(dist, AXES, 0, 0, tiled=True)
-    coarse = jnp.sum(coarse, axis=0)
+    for bit in range(log2(groups)):
+        pairs = [(g, g ^ (1 << bit)) for g in range(groups)]
+        coarse = coarse + lax.ppermute(away, "grp", pairs)
+        if bit < log2(groups) - 1:
+            half = coarse.shape[0] // 2
+            coarse, away = coarse[:half], coarse[half:]
     coarse_new = (coarse_old + coarse[:, :width]) / (1.0 + coarse[:, width : width + 1])
     distances = call(
         functools.partial(finish_kernel, dests=dests),

time: 116 us -> 110 us (0.948)
  local copies, waits for them, and re-layouts: 4.18 us -> 0.02 us
  waiting for transfers between devices: 5.89 us -> 2.97 us
    all_to_all x1 -> x0, waiting for transfers between devices: 5.89 us -> none  [on_device(): lax.all_to_all(coarse.reshape(groups, kc // groups, width + LANES), 'grp'...]
    ppermute x0 -> x3, starting transfers between devices: none -> 4.78 us  [on_device(): coarse = coarse + lax.ppermute(away, 'grp', pairs)]
    unnamed x12 -> x4, local copies, waits for them, and re-layouts: 4.18 us -> 0.01 us
    all_to_all x1 -> x0, starting transfers between devices: 3.78 us -> none  [on_device(): lax.all_to_all(coarse.reshape(groups, kc // groups, width + LANES), 'grp'...]
    ppermute x0 -> x3, waiting for transfers between devices: none -> 2.97 us  [on_device(): coarse = coarse + lax.ppermute(away, 'grp', pairs)]
    pallas_call x2, Pallas kernels: 7.25 us -> 5.87 us  [the longest x1 3.63 us: on_device(): call(functools.partial(distance_kernel, dests=dests), (shape((dests, SLOT...]
  transfers between devices with their start and end apart: 1 -> 3, of which waited for: 1 -> 2; matrix products, arithmetic and copies ran while one was open for 0% -> 0% of each run, Pallas kernels for 1% -> 4%
where the time goes in v2:
time: 110 us
  blocking collectives  91.3 us (83%)
  Pallas kernels  9.46 us (9%)
  starting transfers between devices  4.78 us (4%)
  waiting for transfers between devices  2.97 us (3%)
    all_to_all x1, blocking collectives, on_device(): lax.all_to_all(msg.reshape(dests, per_msg // 2, 2, LANES), AXES, 0, 0, ti...  71.6 us
    all_to_all x1, blocking collectives, on_device(): back = lax.all_to_all(dist, AXES, 0, 0, tiled=True)  19.7 us
    ppermute x3, starting transfers between devices, on_device(): coarse = coarse + lax.ppermute(away, 'grp', pairs)  4.78 us
    pallas_call x1, Pallas kernels, on_device(): call(functools.partial(distance_kernel, dests=dests), (shape((dests, SLOT...  3.63 us
    ppermute x3, waiting for transfers between devices, on_device(): coarse = coarse + lax.ppermute(away, 'grp', pairs)  2.97 us
    pallas_call x1, Pallas kernels, on_device(): call(functools.partial(pack_kernel, dests=dests, groups=groups, kc=kc, fg...  2.67 us
    pallas_call x1, Pallas kernels, on_device(): call(functools.partial(update_kernel, dests=dests, groups=groups, kc=kc,...  2.24 us
  transfers between devices with their start and end apart: 3, of which 2 were waited for; matrix products, arithmetic and copies ran while one was open for 0% of the time, Pallas kernels for 4%

profile of v2, /device:TPU:1, one launch (start us, length us, event | category | flops | bytes accessed | tf_op | source)
XLA Modules:
  0.0 110.1 jit_solution(8023924986539090014)
XLA Ops:
  0.6 2.7 %shard_map.76 = (bf16[8704,128]{1,0:T(8,128)(2,1)S(1)}, s32[1,512]{1,0:T(1,128)S(1)}) custom-call(s32[1,512]{1,0:T(1,128)} %bitcast.16, s32[1,512]{1,0:T(1,128)} %bitcast.17, bf16[512,1024]{1,0:T(8,128)(2,1)} %emb_hbm.1), custom_call_target="tpu_custom_call" | custom-call | tf_op jit(solution)/shard_map/pallas_call | solution.py:188
  3.3 0.0 copy-start
  3.3 71.6 %all_to_all.16 = bf16[256,17,2,128]{3,2,1,0:T(2,128)(2,1)S(1)} all-to-all(bf16[256,17,2,128]{3,2,1,0:T(2,128)(2,1)S(1)} %bitcast.12), channel_id=1, replica_groups=mesh['rows'=32,'grp'=8] {'rows','grp'}, dimensions={0} | all-to-all | bytes 4456448 | tf_op jit(solution)/shard_map/all_to_all | solution.py:201
  74.9 0.0 copy-done
  74.9 2.2 %shard_map.77 = (f32[512,1024]{1,0:T(8,128)S(1)}, f32[32,1152]{1,0:T(8,128)S(1)}, f32[32,1152]{1,0:T(8,128)S(1)}, bf16[1024,1024]{1,0:T(8,128)(2,1)S(1)}, f32[256,128]{1,0:T(8,128)S(1)}) custom-call(bf16[8704,128]{1,0:T(8,128)(2,1)S(1)} %bitcast.11, f32[512,1024]{1,0:T(8,128)S(1)} %bitcast.13), custom_call_target="tpu_custom_call" | custom-call | tf_op jit(solution)/shard_map/pallas_call | solution.py:202
  77.2 0.9 collective-permute-start
  78.1 1.0 collective-permute-done
  79.1 1.3 %collective-permute-start.1 = (f32[16,1152]{1,0:T(8,128)S(1)}, f32[16,1152]{1,0:T(8,128)S(1)}, u32[]{:S(2)}, u32[]{:S(2)}) collective-permute-start(f32[16,1152]{1,0:T(8,128)S(1)} %slice.25), channel_id=1, source_target_pairs={{0,2},{1,3},{2,0},{3,1},{4,6},{5,7},{6,4},{7,5},{8,10},{9,11},{10,... | collective-permute-start | bytes 221192 | tf_op jit(solution)/shard_map/ppermute | solution.py:222
  80.4 2.0 %collective-permute-done.1 = f32[16,1152]{1,0:T(8,128)S(1)} collective-permute-done((f32[16,1152]{1,0:T(8,128)S(1)}, f32[16,1152]{1,0:T(8,128)S(1)}, u32[]{:S(2)}, u32[]{:S(2)}) %collective-permute-start.1) | collective-permute-done | bytes 73760 | tf_op jit(solution)/shard_map/ppermute | solution.py:222
  82.4 2.6 %collective-permute-start.2 = (f32[8,1152]{1,0:T(8,128)S(1)}, f32[8,1152]{1,0:T(8,128)S(1)}, u32[]{:S(2)}, u32[]{:S(2)}) collective-permute-start(f32[8,1152]{1,0:T(8,128)S(1)} %slice.27), channel_id=1, source_target_pairs={{0,4},{1,5},{2,6},{3,7},{4,0},{5,1},{6,2},{7,3},{8,12},{9,13},{10,... | collective-permute-start | bytes 110600 | tf_op jit(solution)/shard_map/ppermute | solution.py:222
  85.0 0.0 copy-start.1
  85.0 3.6 %shard_map.78 = (f32[256,4]{1,0:T(8,128)S(1)}, f32[512,1024]{1,0:T(8,128)}) custom-call(bf16[1024,1024]{1,0:T(8,128)(2,1)S(1)} %get-tuple-element.15.x_ref, f32[512,1024]{1,0:T(8,128)S(1)} %get-tuple-element.16.new_ref, f32[256,128]{1,0:T(8,128)S(1)} %get-tuple-element.17.key_ref), custom_call_target="tpu_custom_call" | custom-call | tf_op jit(solution)/shard_map/pallas_call | solution.py:213
  88.6 19.7 %all_to_all.17 = f32[256,1,4]{2,1,0:T(1,128)S(1)} all-to-all(f32[256,1,4]{2,1,0:T(1,128)S(1)} %bitcast.15), channel_id=1, replica_groups=mesh['rows'=32,'grp'=8] {'rows','grp'}, dimensions={0} | all-to-all | bytes 8192 | tf_op jit(solution)/shard_map/all_to_all | solution.py:219
  108.4 0.9 shard_map.79
  109.3 0.0 collective-permute-done.2
  109.3 0.1 fusion.1
  109.4 0.0 copy-done.1
  109.4 0.7 fusion
  (5 shorter events, 0.0 us)
Async XLA Ops:
  3.3 71.6 %copy-start = (f32[64,8,1024]{2,1,0:T(8,128)S(1)}, f32[64,8,1024]{2,1,0:T(8,128)}, u32[]{:S(2)}) copy-start(f32[64,8,1024]{2,1,0:T(8,128)} %param.9) | copy-start | bytes 6291460
  77.2 1.9 %collective-permute-start = (f32[32,1152]{1,0:T(8,128)S(1)}, f32[32,1152]{1,0:T(8,128)S(1)}, u32[]{:S(2)}, u32[]{:S(2)}) collective-permute-start(f32[32,1152]{1,0:T(8,128)S(1)} %get-tuple-element.14), channel_id=1, source_target_pairs={{0,1},{1,0},{2,3},{3,2},{4,5},{5,4},{6,7},{7,6},{8,9},{9,8},{10,11... | collective-permute-start | bytes 442376 | tf_op jit(solution)/shard_map/ppermute | solution.py:222
  79.1 3.3 %collective-permute-start.1 = (f32[16,1152]{1,0:T(8,128)S(1)}, f32[16,1152]{1,0:T(8,128)S(1)}, u32[]{:S(2)}, u32[]{:S(2)}) collective-permute-start(f32[16,1152]{1,0:T(8,128)S(1)} %slice.25), channel_id=1, source_target_pairs={{0,2},{1,3},{2,0},{3,1},{4,6},{5,7},{6,4},{7,5},{8,10},{9,11},{10,... | collective-permute-start | bytes 221192 | tf_op jit(solution)/shard_map/ppermute | solution.py:222
  82.4 26.8 %collective-permute-start.2 = (f32[8,1152]{1,0:T(8,128)S(1)}, f32[8,1152]{1,0:T(8,128)S(1)}, u32[]{:S(2)}, u32[]{:S(2)}) collective-permute-start(f32[8,1152]{1,0:T(8,128)S(1)} %slice.27), channel_id=1, source_target_pairs={{0,4},{1,5},{2,6},{3,7},{4,0},{5,1},{6,2},{7,3},{8,12},{9,13},{10,... | collective-permute-start | bytes 110600 | tf_op jit(solution)/shard_map/ppermute | solution.py:222
  85.0 24.4 %copy-start.1 = (f32[8,1024]{1,0:T(8,128)S(1)}, f32[8,1024]{1,0:T(8,128)}, u32[]{:S(2)}) copy-start(f32[8,1024]{1,0:T(8,128)} %param.8) | copy-start | bytes 98308

commit v3 on v2

--- a/solution.py
+++ b/solution.py
@@ -86,7 +86,28 @@
     msg_ref[...] = wide_ref[...].astype(jnp.bfloat16)
 
 
-def update_kernel(msg_ref, old_ref, new_ref, keep_ref, send_ref, x_ref, key_ref, wide_ref, mem_ref, *, dests, groups, kc, fg):
+def update_kernel(
+    msg_ref,
+    old_ref,
+    keep_ref,
+    send_ref,
+    dist_ref,
+    out_hbm,
+    wide_ref,
+    x_ref,
+    mem_ref,
+    new_ref,
+    tall_ref,
+    key_ref,
+    key_smem,
+    gap_ref,
+    sems,
+    *,
+    dests,
+    groups,
+    kc,
+    fg,
+):
     cells, width = old_ref.shape
     lane_groups = width // LANES
     per_msg = SLOTS * lane_groups + 2
@@ -94,10 +115,11 @@
     wide_ref[...] = msg_ref[...].astype(jnp.float32)
     high = wide_ref[pl.ds(SLOTS * lane_groups, dests, stride=per_msg), :]
     low = wide_ref[pl.ds(SLOTS * lane_groups + 1, dests, stride=per_msg), :]
-    key = high * fg + low
-    key_ref[...] = key
-    across = jnp.transpose(key)
-    keys = jnp.concatenate([across[s : s + 1, :] for s in range(SLOTS)], axis=1).astype(jnp.int32)
+    across = jnp.transpose(high * fg + low)[:8].astype(jnp.int32)
+    key_ref[...] = jnp.minimum(jnp.maximum(across, 0), cells - 1)
+    key_copy = pltpu.make_async_copy(key_ref, key_smem, sems.at[0])
+    key_copy.start()
+    keys = jnp.concatenate([across[s : s + 1, :] for s in range(SLOTS)], axis=1)
     for s in range(SLOTS):
         for g in range(lane_groups):
             part = wide_ref[pl.ds(s * lane_groups + g, dests, stride=per_msg), :]
@@ -118,41 +140,34 @@
     for n in range(width // step):
         at = slice(n * step, (n + 1) * step)
         sums = jnp.dot(mem_ref[...], x_ref[:, at], preferred_element_type=jnp.float32)
-        new_ref[:, at] = (old_ref[:, at] + sums[:cells]) / (1.0 + counts)
+        new = (old_ref[:, at] + sums[:cells]) / (1.0 + counts)
+        new_ref[:, at] = new
+        for h in range(2):
+            tall_ref[pl.ds(2 * n + h, cells, stride=lane_groups), :] = new[:, h * LANES : (h + 1) * LANES]
         keep_ref[:, at] = sums[cells : cells + kc // 2]
         send_ref[:, at] = sums[cells + kc // 2 :]
-
-
-def distance_kernel(x_ref, new_ref, key_ref, dist_ref, out_hbm, hot_ref, acc_ref, sem, *, dests):
-    out_copy = pltpu.make_async_copy(new_ref, out_hbm, sem)
+    out_copy = pltpu.make_async_copy(new_ref, out_hbm, sems.at[1])
     out_copy.start()
-    cells, width = new_ref.shape
-    key = key_ref[...].astype(jnp.int32)
-    for s in range(SLOTS):
-        hit = iota((dests, cells), 1) == key[:, s : s + 1]
-        hot_ref[s * dests : (s + 1) * dests, :] = jnp.where(hit, 1.0, 0.0).astype(jnp.bfloat16)
-    step = 2 * LANES
-    for n in range(width // step):
-        at = slice(n * step, (n + 1) * step)
-        new = new_ref[:, at]
-        top = new.astype(jnp.bfloat16)
-        rest = new - top.astype(jnp.float32)
-        mid = rest.astype(jnp.bfloat16)
-        end = (rest - mid.astype(jnp.float32)).astype(jnp.bfloat16)
-        hot = hot_ref[...]
-        picked = jnp.dot(hot, top, preferred_element_type=jnp.float32)
-        picked += jnp.dot(hot, mid, preferred_element_type=jnp.float32)
-        picked += jnp.dot(hot, end, preferred_element_type=jnp.float32)
-        diff = x_ref[:, at].astype(jnp.float32) - picked
-        diff = diff * diff
-        both = diff[:, :LANES] + diff[:, LANES:]
-        if n == 0:
-            acc_ref[...] = both
-        else:
-            acc_ref[...] += both
-    for s in range(SLOTS):
-        total = jnp.sum(acc_ref[s * dests : (s + 1) * dests, :], axis=1, keepdims=True)
-        dist_ref[:, s : s + 1] = total * (1.0 / width)
+    key_copy.wait()
+    unroll = 8
+
+    @pl.loop(0, dests // unroll)
+    def _(i):
+        base = pl.multiple_of(i * (unroll * per_msg), 8)
+        for u in range(unroll):
+            for s in range(SLOTS):
+                key = key_smem[s, i * unroll + u]
+                near = tall_ref[pl.ds(pl.multiple_of(key * lane_groups, 8), lane_groups), :]
+                row = wide_ref[pl.ds(base + u * per_msg + s * lane_groups, lane_groups), :]
+                gap = row - near
+                at = (s * dests + u) * lane_groups + i * (unroll * lane_groups)
+                gap_ref[pl.ds(pl.multiple_of(at, 8), lane_groups), :] = gap * gap
+
+    for s in range(SLOTS):
+        total = gap_ref[pl.ds(s * dests * lane_groups, dests, stride=lane_groups), :]
+        for j in range(1, lane_groups):
+            total += gap_ref[pl.ds(s * dests * lane_groups + j, dests, stride=lane_groups), :]
+        dist_ref[:, s : s + 1] = jnp.sum(total, axis=1, keepdims=True) * (1.0 / width)
     out_copy.wait()
 
 
@@ -199,30 +214,37 @@
         in_specs=[pl.BlockSpec(memory_space=pltpu.HBM)] * 3,
     )(*(pltpu.with_memory_space_constraint(a, pltpu.HBM) for a in (ids[0], ids[1], embeddings)))
     msg = lax.all_to_all(msg.reshape(dests, per_msg // 2, 2, LANES), AXES, 0, 0, tiled=True)
-    new, coarse, away, x, key = call(
+    coarse, away, dist, new = call(
         functools.partial(update_kernel, dests=dests, groups=groups, kc=kc, fg=fg),
         (
-            shape((cells, width), f32),
             shape((kc // 2, width + LANES), f32),
             shape((kc // 2, width + LANES), f32),
-            shape((slots, width), bf16),
-            shape((dests, LANES), f32),
-        ),
-        (pltpu.VMEM((dests * per_msg, LANES), f32), pltpu.VMEM((cells + kc, slots), bf16)),
+            shape((dests, SLOTS), f32),
+            shape((cells, width), f32),
+        ),
+        (
+            pltpu.VMEM((dests * per_msg, LANES), f32),
+            pltpu.VMEM((slots, width), bf16),
+            pltpu.VMEM((cells + kc, slots), bf16),
+            pltpu.VMEM((cells, width), f32),
+            pltpu.VMEM((cells * width // LANES, LANES), f32),
+            pltpu.VMEM((8, dests), jnp.int32),
+            pltpu.SMEM((8, dests), jnp.int32),
+            pltpu.VMEM((slots * width // LANES, LANES), f32),
+            pltpu.SemaphoreType.DMA((2,)),
+        ),
+        32 << 20,
+        out_specs=(pl.BlockSpec(memory_space=pltpu.VMEM),) * 3 + (pl.BlockSpec(memory_space=pltpu.HBM),),
     )(msg.reshape(dests * per_msg, LANES), fine_old.reshape(cells, width))
-    dist, new = call(
-        functools.partial(distance_kernel, dests=dests),
-        (shape((dests, SLOTS), f32), shape((cells, width), f32)),
-        (pltpu.VMEM((slots, cells), bf16), pltpu.VMEM((slots, LANES), f32), pltpu.SemaphoreType.DMA(())),
-        out_specs=(pl.BlockSpec(memory_space=pltpu.VMEM), pl.BlockSpec(memory_space=pltpu.HBM)),
-    )(x, new, key)
     back = lax.all_to_all(dist, AXES, 0, 0, tiled=True)
-    for bit in range(log2(groups)):
-        pairs = [(g, g ^ (1 << bit)) for g in range(groups)]
-        coarse = coarse + lax.ppermute(away, "grp", pairs)
-        if bit < log2(groups) - 1:
-            half = coarse.shape[0] // 2
-            coarse, away = coarse[:half], coarse[half:]
+    rounds = log2(groups)
+    coarse = coarse + lax.ppermute(away, "grp", [(g, g ^ 1) for g in range(groups)])
+    owned = kc // groups
+    parts = [coarse[:owned]]
+    for p in range(1, groups // 2):
+        partner = sum(((p >> b) & 1) << (rounds - 1 - b) for b in range(rounds))
+        parts.append(lax.ppermute(coarse[p * owned : (p + 1) * owned], "grp", [(g, g ^ partner) for g in range(groups)]))
+    coarse = functools.reduce(jnp.add, parts)
     coarse_new = (coarse_old + coarse[:, :width]) / (1.0 + coarse[:, width : width + 1])
     distances = call(
         functools.partial(finish_kernel, dests=dests),

time: 110 us -> 107 us (0.973)
  waiting for transfers between devices: 2.97 us -> 1.02 us
    pallas_call x1 -> x0, Pallas kernels: 3.63 us -> none  [on_device(): call(functools.partial(distance_kernel, dests=dests), (shape((dests, SLOT...]
    pallas_call x1, Pallas kernels: 2.24 us -> 4.84 us  [on_device(): call(functools.partial(update_kernel, dests=dests, groups=groups, kc=kc,...]
    ppermute x3 -> x4, waiting for transfers between devices: 2.97 us -> 1.02 us  [the longest x1 1.01 us: on_device(): lax.ppermute(away, 'grp', [(g, g ^ 1) for g in range(groups)])]
    ppermute x3 -> x4, starting transfers between devices: 4.78 us -> 4.6 us  [the longest x3 3.73 us: on_device(): lax.ppermute(coarse[p * owned:(p + 1) * owned], 'grp', [(g, g ^ partner)...]
  transfers between devices with their start and end apart: 3 -> 4, of which waited for: 2 -> 1; matrix products, arithmetic and copies ran while one was open for 0% -> 0% of each run, Pallas kernels for 4% -> 1%
where the time goes in v3:
time: 107 us
  blocking collectives  90.9 us (85%)
  Pallas kernels  8.43 us (8%)
  starting transfers between devices  4.6 us (4%)
    all_to_all x1, blocking collectives, on_device(): lax.all_to_all(msg.reshape(dests, per_msg // 2, 2, LANES), AXES, 0, 0, ti...  71.6 us
    all_to_all x1, blocking collectives, on_device(): back = lax.all_to_all(dist, AXES, 0, 0, tiled=True)  19.3 us
    pallas_call x1, Pallas kernels, on_device(): call(functools.partial(update_kernel, dests=dests, groups=groups, kc=kc,...  4.84 us
    ppermute x3, starting transfers between devices, on_device(): lax.ppermute(coarse[p * owned:(p + 1) * owned], 'grp', [(g, g ^ partner)...  3.73 us
    pallas_call x1, Pallas kernels, on_device(): call(functools.partial(pack_kernel, dests=dests, groups=groups, kc=kc, fg...  2.67 us
  transfers between devices with their start and end apart: 4, of which 1 were waited for; matrix products, arithmetic and copies ran while one was open for 0% of the time, Pallas kernels for 1%

profile of v3, /device:TPU:1, one launch (start us, length us, event | category | flops | bytes accessed | tf_op | source)
XLA Modules:
  0.0 106.5 jit_solution(14158819579561716324)
XLA Ops:
  0.6 2.7 %shard_map.76 = (bf16[8704,128]{1,0:T(8,128)(2,1)S(1)}, s32[1,512]{1,0:T(1,128)S(1)}) custom-call(s32[1,512]{1,0:T(1,128)} %bitcast.16, s32[1,512]{1,0:T(1,128)} %bitcast.17, bf16[512,1024]{1,0:T(8,128)(2,1)} %emb_hbm.1), custom_call_target="tpu_custom_call" | custom-call | tf_op jit(solution)/shard_map/pallas_call | solution.py:203
  3.3 0.0 copy-start
  3.3 71.6 %all_to_all.16 = bf16[256,17,2,128]{3,2,1,0:T(2,128)(2,1)S(1)} all-to-all(bf16[256,17,2,128]{3,2,1,0:T(2,128)(2,1)S(1)} %bitcast.12), channel_id=1, replica_groups=mesh['rows'=32,'grp'=8] {'rows','grp'}, dimensions={0} | all-to-all | bytes 4456448 | tf_op jit(solution)/shard_map/all_to_all | solution.py:216
  74.9 0.0 copy-done
  74.9 0.0 copy-start.1
  74.9 4.8 %shard_map.77 = (f32[32,1152]{1,0:T(8,128)S(1)}, f32[32,1152]{1,0:T(8,128)S(1)}, f32[256,4]{1,0:T(8,128)S(1)}, f32[512,1024]{1,0:T(8,128)}) custom-call(bf16[8704,128]{1,0:T(8,128)(2,1)S(1)} %bitcast.11, f32[512,1024]{1,0:T(8,128)S(1)} %bitcast.13), custom_call_target="tpu_custom_call" | custom-call | tf_op jit(solution)/shard_map/pallas_call | solution.py:217
  79.8 0.9 collective-permute-start
  80.7 1.0 collective-permute-done
  81.7 2.6 %collective-permute-start.1 = (f32[8,1152]{1,0:T(8,128)S(1)}, f32[8,1152]{1,0:T(8,128)S(1)}, u32[]{:S(2)}, u32[]{:S(2)}) collective-permute-start(f32[8,1152]{1,0:T(8,128)S(1)} %get-tuple-element.15), channel_id=1, source_target_pairs={{0,4},{1,5},{2,6},{3,7},{4,0},{5,1},{6,2},{7,3},{8,12},{9,13},{10,... | collective-permute-start | bytes 110600 | tf_op jit(solution)/shard_map/ppermute | solution.py:246
  84.3 1.2 %collective-permute-start.3 = (f32[8,1152]{1,0:T(8,128)S(1)}, f32[8,1152]{1,0:T(8,128)S(1)}, u32[]{:S(2)}, u32[]{:S(2)}) collective-permute-start(f32[8,1152]{1,0:T(8,128)S(1)} %get-tuple-element.16), channel_id=1, source_target_pairs={{0,6},{1,7},{2,4},{3,5},{4,2},{5,3},{6,0},{7,1},{8,14},{9,15},{10,... | collective-permute-start | bytes 110600 | tf_op jit(solution)/shard_map/ppermute | solution.py:246
  85.4 0.0 collective-permute-start.2
  85.4 19.3 %all_to_all.17 = f32[256,1,4]{2,1,0:T(1,128)S(1)} all-to-all(f32[256,1,4]{2,1,0:T(1,128)S(1)} %bitcast.15), channel_id=1, replica_groups=mesh['rows'=32,'grp'=8] {'rows','grp'}, dimensions={0} | all-to-all | bytes 8192 | tf_op jit(solution)/shard_map/all_to_all | solution.py:239
  104.7 0.9 shard_map.78
  105.7 0.0 collective-permute-done.1
  105.7 0.0 collective-permute-done.3
  105.7 0.0 collective-permute-done.2
  105.7 0.1 fusion.3
  105.8 0.0 copy-done.1
  105.8 0.7 fusion.2
  (3 shorter events, 0.0 us)
Async XLA Ops:
  3.3 71.6 %copy-start = (f32[64,8,1024]{2,1,0:T(8,128)S(1)}, f32[64,8,1024]{2,1,0:T(8,128)}, u32[]{:S(2)}) copy-start(f32[64,8,1024]{2,1,0:T(8,128)} %param.9) | copy-start | bytes 6291460
  74.9 30.9 %copy-start.1 = (f32[8,1024]{1,0:T(8,128)S(1)}, f32[8,1024]{1,0:T(8,128)}, u32[]{:S(2)}) copy-start(f32[8,1024]{1,0:T(8,128)} %param.8) | copy-start | bytes 98308
  79.8 1.9 %collective-permute-start = (f32[32,1152]{1,0:T(8,128)S(1)}, f32[32,1152]{1,0:T(8,128)S(1)}, u32[]{:S(2)}, u32[]{:S(2)}) collective-permute-start(f32[32,1152]{1,0:T(8,128)S(1)} %get-tuple-element.11), channel_id=1, source_target_pairs={{0,1},{1,0},{2,3},{3,2},{4,5},{5,4},{6,7},{7,6},{8,9},{9,8},{10,11... | collective-permute-start | bytes 442376 | tf_op jit(solution)/shard_map/ppermute | solution.py:241
  81.7 24.0 %collective-permute-start.1 = (f32[8,1152]{1,0:T(8,128)S(1)}, f32[8,1152]{1,0:T(8,128)S(1)}, u32[]{:S(2)}, u32[]{:S(2)}) collective-permute-start(f32[8,1152]{1,0:T(8,128)S(1)} %get-tuple-element.15), channel_id=1, source_target_pairs={{0,4},{1,5},{2,6},{3,7},{4,0},{5,1},{6,2},{7,3},{8,12},{9,13},{10,... | collective-permute-start | bytes 110600 | tf_op jit(solution)/shard_map/ppermute | solution.py:246
  84.3 21.4 %collective-permute-start.3 = (f32[8,1152]{1,0:T(8,128)S(1)}, f32[8,1152]{1,0:T(8,128)S(1)}, u32[]{:S(2)}, u32[]{:S(2)}) collective-permute-start(f32[8,1152]{1,0:T(8,128)S(1)} %get-tuple-element.16), channel_id=1, source_target_pairs={{0,6},{1,7},{2,4},{3,5},{4,2},{5,3},{6,0},{7,1},{8,14},{9,15},{10,... | collective-permute-start | bytes 110600 | tf_op jit(solution)/shard_map/ppermute | solution.py:246
  85.4 20.2 %collective-permute-start.2 = (f32[8,1152]{1,0:T(8,128)S(1)}, f32[8,1152]{1,0:T(8,128)S(1)}, u32[]{:S(2)}, u32[]{:S(2)}) collective-permute-start(f32[8,1152]{1,0:T(8,128)S(1)} %get-tuple-element.17), channel_id=1, source_target_pairs={{0,2},{1,3},{2,0},{3,1},{4,6},{5,7},{6,4},{7,5},{8,10},{9,11},{10,... | collective-permute-start | bytes 110600 | tf_op jit(solution)/shard_map/ppermute | solution.py:246

commit v4 on v3

--- a/solution.py
+++ b/solution.py
@@ -86,6 +86,22 @@
     msg_ref[...] = wide_ref[...].astype(jnp.bfloat16)
 
 
+def fold(parts):
+    parts = [parts[u ^ 3] for u in range(8)]
+    row = iota(parts[0].shape, 0)
+    low = row < 4
+    parts = [
+        jnp.where(low, a, b) + pltpu.roll(jnp.where(low, b, a), 4, 0) for a, b in zip(parts[:4], parts[4:])
+    ]
+    for k in (2, 1):
+        kept = (row & k) != 0
+        parts = [
+            jnp.where(kept, a, b) + jnp.where(kept, pltpu.roll(a, k, 0), pltpu.roll(b, 8 - k, 0))
+            for a, b in zip(parts[:k], parts[k:])
+        ]
+    return parts[0]
+
+
 def update_kernel(
     msg_ref,
     old_ref,
@@ -98,6 +114,7 @@
     mem_ref,
     new_ref,
     tall_ref,
+    column_ref,
     key_ref,
     key_smem,
     gap_ref,
@@ -115,10 +132,20 @@
     wide_ref[...] = msg_ref[...].astype(jnp.float32)
     high = wide_ref[pl.ds(SLOTS * lane_groups, dests, stride=per_msg), :]
     low = wide_ref[pl.ds(SLOTS * lane_groups + 1, dests, stride=per_msg), :]
-    across = jnp.transpose(high * fg + low)[:8].astype(jnp.int32)
-    key_ref[...] = jnp.minimum(jnp.maximum(across, 0), cells - 1)
+    key = high * fg + low
+    column_ref[...] = jnp.minimum(jnp.maximum(key.astype(jnp.int32), 0), cells - 1) * lane_groups
+    unroll = 16
+    steps = dests // unroll
+    near = jnp.zeros((steps, LANES), jnp.int32)
+    for u in range(unroll):
+        part = column_ref[pl.ds(u, steps, stride=unroll), :]
+        if u:
+            part = pltpu.roll(part, u * SLOTS, 1)
+        near = jnp.where(iota((steps, LANES), 1) >> log2(SLOTS) == u, part, near)
+    key_ref[...] = near
     key_copy = pltpu.make_async_copy(key_ref, key_smem, sems.at[0])
     key_copy.start()
+    across = jnp.transpose(key)[:8].astype(jnp.int32)
     keys = jnp.concatenate([across[s : s + 1, :] for s in range(SLOTS)], axis=1)
     for s in range(SLOTS):
         for g in range(lane_groups):
@@ -149,25 +176,23 @@
     out_copy = pltpu.make_async_copy(new_ref, out_hbm, sems.at[1])
     out_copy.start()
     key_copy.wait()
-    unroll = 8
-
-    @pl.loop(0, dests // unroll)
+
+    @pl.loop(0, steps)
     def _(i):
         base = pl.multiple_of(i * (unroll * per_msg), 8)
-        for u in range(unroll):
-            for s in range(SLOTS):
-                key = key_smem[s, i * unroll + u]
-                near = tall_ref[pl.ds(pl.multiple_of(key * lane_groups, 8), lane_groups), :]
-                row = wide_ref[pl.ds(base + u * per_msg + s * lane_groups, lane_groups), :]
-                gap = row - near
-                at = (s * dests + u) * lane_groups + i * (unroll * lane_groups)
-                gap_ref[pl.ds(pl.multiple_of(at, 8), lane_groups), :] = gap * gap
-
-    for s in range(SLOTS):
-        total = gap_ref[pl.ds(s * dests * lane_groups, dests, stride=lane_groups), :]
-        for j in range(1, lane_groups):
-            total += gap_ref[pl.ds(s * dests * lane_groups + j, dests, stride=lane_groups), :]
-        dist_ref[:, s : s + 1] = jnp.sum(total, axis=1, keepdims=True) * (1.0 / width)
+        for s in range(SLOTS):
+            for v in range(0, unroll, 8):
+                gaps = []
+                for u in range(v, v + 8):
+                    at = pl.multiple_of(key_smem[i, u * SLOTS + s], 8)
+                    row = wide_ref[pl.ds(base + u * per_msg + s * lane_groups, lane_groups), :]
+                    gap = row - tall_ref[pl.ds(at, lane_groups), :]
+                    gaps.append(gap * gap)
+                gap_ref[pl.ds(pl.multiple_of(s * dests + i * unroll + v, 8), 8), :] = fold(gaps)
+
+    for s in range(SLOTS):
+        total = jnp.sum(gap_ref[s * dests : (s + 1) * dests, :], axis=1, keepdims=True)
+        dist_ref[:, s : s + 1] = total * (1.0 / width)
     out_copy.wait()
 
 
@@ -228,9 +253,10 @@
             pltpu.VMEM((cells + kc, slots), bf16),
             pltpu.VMEM((cells, width), f32),
             pltpu.VMEM((cells * width // LANES, LANES), f32),
-            pltpu.VMEM((8, dests), jnp.int32),
-            pltpu.SMEM((8, dests), jnp.int32),
-            pltpu.VMEM((slots * width // LANES, LANES), f32),
+            pltpu.VMEM((dests, LANES), jnp.int32),
+            pltpu.VMEM((dests // 16, LANES), jnp.int32),
+            pltpu.SMEM((dests // 16, LANES), jnp.int32),
+            pltpu.VMEM((slots, LANES), f32),
             pltpu.SemaphoreType.DMA((2,)),
         ),
         32 << 20,

time: 107 us -> 106 us (level)
  no operation moved by 1% of the time
where the time goes in v4:
time: 106 us; the launch traced here: 105 us
  blocking collectives  90.9 us (86%)
  Pallas kernels  7.37 us (7%)
  starting transfers between devices  4.61 us (4%)
    all_to_all x1, blocking collectives, on_device(): lax.all_to_all(msg.reshape(dests, per_msg // 2, 2, LANES), AXES, 0, 0, ti...  71.6 us
    all_to_all x1, blocking collectives, on_device(): back = lax.all_to_all(dist, AXES, 0, 0, tiled=True)  19.3 us
    pallas_call x1, Pallas kernels, on_device(): call(functools.partial(update_kernel, dests=dests, groups=groups, kc=kc,...  3.78 us
    ppermute x3, starting transfers between devices, on_device(): lax.ppermute(coarse[p * owned:(p + 1) * owned], 'grp', [(g, g ^ partner)...  3.74 us
    pallas_call x1, Pallas kernels, on_device(): call(functools.partial(pack_kernel, dests=dests, groups=groups, kc=kc, fg...  2.67 us
  transfers between devices with their start and end apart: 4, of which 1 were waited for; matrix products, arithmetic and copies ran while one was open for 0% of the time, Pallas kernels for 1%

profile of v4, /device:TPU:1, one launch (start us, length us, event | category | flops | bytes accessed | tf_op | source)
XLA Modules:
  0.0 105.5 jit_solution(9383195998716176832)
XLA Ops:
  0.6 2.7 %shard_map.76 = (bf16[8704,128]{1,0:T(8,128)(2,1)S(1)}, s32[1,512]{1,0:T(1,128)S(1)}) custom-call(s32[1,512]{1,0:T(1,128)} %bitcast.16, s32[1,512]{1,0:T(1,128)} %bitcast.17, bf16[512,1024]{1,0:T(8,128)(2,1)} %emb_hbm.1), custom_call_target="tpu_custom_call" | custom-call | tf_op jit(solution)/shard_map/pallas_call | solution.py:228
  3.3 0.0 copy-start
  3.3 71.6 %all_to_all.16 = bf16[256,17,2,128]{3,2,1,0:T(2,128)(2,1)S(1)} all-to-all(bf16[256,17,2,128]{3,2,1,0:T(2,128)(2,1)S(1)} %bitcast.12), channel_id=1, replica_groups=mesh['rows'=32,'grp'=8] {'rows','grp'}, dimensions={0} | all-to-all | bytes 4456448 | tf_op jit(solution)/shard_map/all_to_all | solution.py:241
  74.9 0.0 copy-done
  74.9 0.0 copy-start.1
  74.9 3.8 %shard_map.77 = (f32[32,1152]{1,0:T(8,128)S(1)}, f32[32,1152]{1,0:T(8,128)S(1)}, f32[256,4]{1,0:T(8,128)S(1)}, f32[512,1024]{1,0:T(8,128)}) custom-call(bf16[8704,128]{1,0:T(8,128)(2,1)S(1)} %bitcast.11, f32[512,1024]{1,0:T(8,128)S(1)} %bitcast.13), custom_call_target="tpu_custom_call" | custom-call | tf_op jit(solution)/shard_map/pallas_call | solution.py:242
  78.7 0.9 collective-permute-start
  79.6 1.0 collective-permute-done
  80.7 2.6 %collective-permute-start.1 = (f32[8,1152]{1,0:T(8,128)S(1)}, f32[8,1152]{1,0:T(8,128)S(1)}, u32[]{:S(2)}, u32[]{:S(2)}) collective-permute-start(f32[8,1152]{1,0:T(8,128)S(1)} %get-tuple-element.15), channel_id=1, source_target_pairs={{0,4},{1,5},{2,6},{3,7},{4,0},{5,1},{6,2},{7,3},{8,12},{9,13},{10,... | collective-permute-start | bytes 110600 | tf_op jit(solution)/shard_map/ppermute | solution.py:272
  83.2 1.2 %collective-permute-start.3 = (f32[8,1152]{1,0:T(8,128)S(1)}, f32[8,1152]{1,0:T(8,128)S(1)}, u32[]{:S(2)}, u32[]{:S(2)}) collective-permute-start(f32[8,1152]{1,0:T(8,128)S(1)} %get-tuple-element.16), channel_id=1, source_target_pairs={{0,6},{1,7},{2,4},{3,5},{4,2},{5,3},{6,0},{7,1},{8,14},{9,15},{10,... | collective-permute-start | bytes 110600 | tf_op jit(solution)/shard_map/ppermute | solution.py:272
  84.4 0.0 collective-permute-start.2
  84.4 19.3 %all_to_all.17 = f32[256,1,4]{2,1,0:T(1,128)S(1)} all-to-all(f32[256,1,4]{2,1,0:T(1,128)S(1)} %bitcast.15), channel_id=1, replica_groups=mesh['rows'=32,'grp'=8] {'rows','grp'}, dimensions={0} | all-to-all | bytes 8192 | tf_op jit(solution)/shard_map/all_to_all | solution.py:265
  103.7 0.9 shard_map.78
  104.6 0.0 collective-permute-done.1
  104.6 0.0 collective-permute-done.3
  104.6 0.0 collective-permute-done.2
  104.6 0.1 fusion.3
  104.8 0.0 copy-done.1
  104.8 0.7 fusion.2
  (3 shorter events, 0.0 us)
Async XLA Ops:
  3.3 71.6 %copy-start = (f32[64,8,1024]{2,1,0:T(8,128)S(1)}, f32[64,8,1024]{2,1,0:T(8,128)}, u32[]{:S(2)}) copy-start(f32[64,8,1024]{2,1,0:T(8,128)} %param.9) | copy-start | bytes 6291460
  74.9 29.8 %copy-start.1 = (f32[8,1024]{1,0:T(8,128)S(1)}, f32[8,1024]{1,0:T(8,128)}, u32[]{:S(2)}) copy-start(f32[8,1024]{1,0:T(8,128)} %param.8) | copy-start | bytes 98308
  78.7 1.9 %collective-permute-start = (f32[32,1152]{1,0:T(8,128)S(1)}, f32[32,1152]{1,0:T(8,128)S(1)}, u32[]{:S(2)}, u32[]{:S(2)}) collective-permute-start(f32[32,1152]{1,0:T(8,128)S(1)} %get-tuple-element.11), channel_id=1, source_target_pairs={{0,1},{1,0},{2,3},{3,2},{4,5},{5,4},{6,7},{7,6},{8,9},{9,8},{10,11... | collective-permute-start | bytes 442376 | tf_op jit(solution)/shard_map/ppermute | solution.py:267
  80.7 23.9 %collective-permute-start.1 = (f32[8,1152]{1,0:T(8,128)S(1)}, f32[8,1152]{1,0:T(8,128)S(1)}, u32[]{:S(2)}, u32[]{:S(2)}) collective-permute-start(f32[8,1152]{1,0:T(8,128)S(1)} %get-tuple-element.15), channel_id=1, source_target_pairs={{0,4},{1,5},{2,6},{3,7},{4,0},{5,1},{6,2},{7,3},{8,12},{9,13},{10,... | collective-permute-start | bytes 110600 | tf_op jit(solution)/shard_map/ppermute | solution.py:272
  83.2 21.4 %collective-permute-start.3 = (f32[8,1152]{1,0:T(8,128)S(1)}, f32[8,1152]{1,0:T(8,128)S(1)}, u32[]{:S(2)}, u32[]{:S(2)}) collective-permute-start(f32[8,1152]{1,0:T(8,128)S(1)} %get-tuple-element.16), channel_id=1, source_target_pairs={{0,6},{1,7},{2,4},{3,5},{4,2},{5,3},{6,0},{7,1},{8,14},{9,15},{10,... | collective-permute-start | bytes 110600 | tf_op jit(solution)/shard_map/ppermute | solution.py:272
  84.4 20.2 %collective-permute-start.2 = (f32[8,1152]{1,0:T(8,128)S(1)}, f32[8,1152]{1,0:T(8,128)S(1)}, u32[]{:S(2)}, u32[]{:S(2)}) collective-permute-start(f32[8,1152]{1,0:T(8,128)S(1)} %get-tuple-element.17), channel_id=1, source_target_pairs={{0,2},{1,3},{2,0},{3,1},{4,6},{5,7},{6,4},{7,5},{8,10},{9,11},{10,... | collective-permute-start | bytes 110600 | tf_op jit(solution)/shard_map/ppermute | solution.py:272

commit v5 on v4

v5 whole, which is shorter than its diff:
```python
import functools

import jax
import jax.numpy as jnp
from jax import lax
from jax.experimental import pallas as pl
from jax.experimental.pallas import tpu as pltpu
from jax.sharding import PartitionSpec as P


AXES = ("rows", "grp")
SLOTS = 4
LANES = 128


def log2(n):
    assert n & (n - 1) == 0
    return n.bit_length() - 1


def iota(shape, dim):
    return lax.broadcasted_iota(jnp.int32, shape, dim)


def pack_kernel(
    coarse_hbm,
    fine_hbm,
    emb_hbm,
    msg_ref,
    pos_ref,
    coarse_ref,
    fine_ref,
    emb_ref,
    sems,
    hot_ref,
    wide_ref,
    *,
    dests,
    groups,
    kc,
    fg,
):
    coarse_copy = pltpu.make_async_copy(coarse_hbm, coarse_ref, sems.at[0])
    fine_copy = pltpu.make_async_copy(fine_hbm, fine_ref, sems.at[1])
    emb_copy = pltpu.make_async_copy(emb_hbm, emb_ref, sems.at[2])
    coarse_copy.start()
    fine_copy.start()
    emb_copy.start()
    rows, width = emb_ref.shape
    lane_groups = width // LANES
    per_msg = SLOTS * lane_groups + 2
    part = dests
    coarse_copy.wait()
    fine_copy.wait()
    coarse, fine = coarse_ref[...], fine_ref[...]
    dest = (coarse >> log2(kc)) * groups + (fine >> log2(fg))
    down = jnp.transpose(jnp.broadcast_to(dest, (LANES, rows)))
    ranks = []
    for j in range(0, rows, LANES):
        same = down[: j + LANES] == dest[:, j : j + LANES]
        same = same & (iota((j + LANES, LANES), 0) < iota((j + LANES, LANES), 1) + j)
        ranks.append(jnp.sum(jnp.where(same, 1.0, 0.0), axis=0, keepdims=True))
    rank = jnp.concatenate(ranks, axis=1).astype(jnp.int32)
    pos = rank * dests + dest
    pos_ref[...] = pos
    half = LANES // 2
    names = jnp.where(iota((LANES, rows), 0) < half, (coarse & (kc - 1)) + 1, fine & (fg - 1))
    names = jnp.transpose(names.astype(jnp.float32)).astype(jnp.bfloat16)
    lane = iota((part, LANES), 1)
    step = 2 * LANES
    for p in range(0, dests, part):
        for s in range(SLOTS):
            hit = iota((part, rows), 0) + (s * dests + p) == pos
            hot_ref[p * SLOTS + s * part : p * SLOTS + (s + 1) * part, :] = jnp.where(hit, 1.0, 0.0).astype(jnp.bfloat16)
    for p in range(0, dests, part):
        hot = hot_ref[p * SLOTS : (p + part) * SLOTS, :]
        got = jnp.dot(hot, names, preferred_element_type=jnp.float32)
        named = jnp.zeros((part, LANES), jnp.float32)
        for s in range(SLOTS):
            named = jnp.where(lane & (half - 1) == s, got[s * part : (s + 1) * part], named)
        at = p * per_msg + SLOTS * lane_groups
        wide_ref[pl.ds(at, part, stride=per_msg), :] = named - jnp.where(lane < half, 1.0, 0.0)
        wide_ref[pl.ds(at + 1, part, stride=per_msg), :] = jnp.zeros((part, LANES), jnp.float32)
    emb_copy.wait()
    for p in range(0, dests, part):
        hot = hot_ref[p * SLOTS : (p + part) * SLOTS, :]
        for n in range(width // step):
            got = jnp.dot(hot, emb_ref[:, n * step : (n + 1) * step], preferred_element_type=jnp.float32)
            for h in range(2):
                for s in range(SLOTS):
                    at = p * per_msg + s * lane_groups + 2 * n + h
                    wide_ref[pl.ds(at, part, stride=per_msg), :] = got[s * part : (s + 1) * part, h * LANES : (h + 1) * LANES]
        at = slice(p * per_msg, (p + part) * per_msg)
        msg_ref[at, :] = wide_ref[at, :].astype(jnp.bfloat16)


def fold(parts):
    parts = [parts[u ^ 3] for u in range(8)]
    row = iota(parts[0].shape, 0)
    low = row < 4
    parts = [
        jnp.where(low, a, b) + pltpu.roll(jnp.where(low, b, a), 4, 0) for a, b in zip(parts[:4], parts[4:])
    ]
    for k in (2, 1):
        kept = (row & k) != 0
        parts = [
            jnp.where(kept, a, b) + jnp.where(kept, pltpu.roll(a, k, 0), pltpu.roll(b, 8 - k, 0))
            for a, b in zip(parts[:k], parts[k:])
        ]
    return parts[0]


def update_kernel(
    msg_ref,
    old_ref,
    keep_ref,
    send_ref,
    dist_ref,
    out_hbm,
    wide_ref,
    x_ref,
    mem_ref,
    new_ref,
    tall_ref,
    share_ref,
    column_ref,
    key_ref,
    key_smem,
    gap_ref,
    sems,
    *,
    dests,
    groups,
    kc,
    fg,
):
    cells, width = old_ref.shape
    lane_groups = width // LANES
    per_msg = SLOTS * lane_groups + 2
    slots = SLOTS * dests
    wide_ref[...] = msg_ref[...].astype(jnp.float32)
    names = wide_ref[pl.ds(SLOTS * lane_groups, dests, stride=per_msg), :]
    key = names * fg + pltpu.roll(names, LANES // 2, 1)
    column_ref[...] = jnp.minimum(jnp.maximum(key.astype(jnp.int32), 0), cells - 1) * lane_groups
    unroll = 16
    steps = dests // unroll
    near = jnp.zeros((steps, LANES), jnp.int32)
    for u in range(unroll):
        part = column_ref[pl.ds(u, steps, stride=unroll), :]
        if u:
            part = pltpu.roll(part, u * SLOTS, 1)
        near = jnp.where(iota((steps, LANES), 1) >> log2(SLOTS) == u, part, near)
    key_ref[...] = near
    key_copy = pltpu.make_async_copy(key_ref, key_smem, sems.at[0])
    key_copy.start()
    across = jnp.transpose(key)[:8].astype(jnp.int32)
    keys = jnp.concatenate([across[s : s + 1, :] for s in range(SLOTS)], axis=1)
    for s in range(SLOTS):
        for g in range(lane_groups):
            part = wide_ref[pl.ds(s * lane_groups + g, dests, stride=per_msg), :]
            x_ref[s * dests : (s + 1) * dests, g * LANES : (g + 1) * LANES] = part.astype(jnp.bfloat16)
    member = jnp.where(iota((cells, slots), 0) == keys, 1.0, 0.0)
    mem_ref[:cells, :] = member.astype(jnp.bfloat16)
    block = iota((kc, slots), 0) >> log2(kc // groups)
    block = sum(((block >> b) & 1) << (log2(groups) - 1 - b) for b in range(log2(groups)))
    owned = ((block ^ lax.axis_index("grp")) << log2(kc // groups)) + (iota((kc, slots), 0) & (kc // groups - 1))
    member = jnp.where(owned == (keys >> log2(fg)), 1.0, 0.0)
    mem_ref[cells:, :] = member.astype(jnp.bfloat16)
    ones = jnp.ones((slots, LANES), jnp.bfloat16)
    counts = jnp.dot(mem_ref[...], ones, preferred_element_type=jnp.float32)
    keep_ref[:, width:] = counts[cells : cells + kc // 2]
    send_ref[:, width:] = counts[cells + kc // 2 :]
    share_ref[...] = 1.0 / (1.0 + counts[:cells])
    step = 2 * LANES
    for n in range(width // step):
        at = slice(n * step, (n + 1) * step)
        sums = jnp.dot(mem_ref[...], x_ref[:, at], preferred_element_type=jnp.float32)
        for h in range(2):
            part = slice((2 * n + h) * LANES, (2 * n + h + 1) * LANES)
            new = (old_ref[:, part] + sums[:cells, h * LANES : (h + 1) * LANES]) * share_ref[...]
            new_ref[:, part] = new
            tall_ref[pl.ds(2 * n + h, cells, stride=lane_groups), :] = new
        keep_ref[:, at] = sums[cells : cells + kc // 2]
        send_ref[:, at] = sums[cells + kc // 2 :]
    out_copy = pltpu.make_async_copy(new_ref, out_hbm, sems.at[1])
    out_copy.start()
    key_copy.wait()

    for i in range(steps):
        base = i * (unroll * per_msg)
        for s in range(SLOTS):
            for v in range(0, unroll, 8):
                gaps = []
                for u in range(v, v + 8):
                    at = pl.multiple_of(key_smem[i, u * SLOTS + s], 8)
                    row = wide_ref[pl.ds(base + u * per_msg + s * lane_groups, lane_groups), :]
                    gap = row - tall_ref[pl.ds(at, lane_groups), :]
                    gaps.append(gap * gap)
                gap_ref[pl.ds(s * dests + i * unroll + v, 8), :] = fold(gaps)

    for s in range(SLOTS):
        total = jnp.sum(gap_ref[s * dests : (s + 1) * dests, :], axis=1, keepdims=True)
        dist_ref[:, s : s + 1] = total * (1.0 / width)
    out_copy.wait()


def finish_kernel(back_ref, pos_ref, out_ref, *, dests):
    pos = pos_ref[...]
    dest, rank = pos & (dests - 1), pos >> log2(dests)
    value = back_ref[:, :1]
    for s in range(1, SLOTS):
        value = jnp.where(rank == s, back_ref[:, s : s + 1], value)
    hit = iota((dests, pos.shape[1]), 0) == dest
    out_ref[...] = jnp.sum(jnp.where(hit, value, 0.0), axis=0, keepdims=True)


def call(kernel, outs, scratch=(), limit=24 << 20, **specs):
    return pl.pallas_call(
        kernel,
        out_shape=outs,
        **specs,
        scratch_shapes=list(scratch),
        compiler_params=pltpu.CompilerParams(vmem_limit_bytes=limit),
    )


def pack(coarse_ids, fine_ids, embeddings, dests, groups, kc, fg):
    rows, width = embeddings.shape
    per_msg = SLOTS * (width // LANES) + 2
    f32, bf16, shape = jnp.float32, jnp.bfloat16, jax.ShapeDtypeStruct
    ids = coarse_ids.reshape(1, rows), fine_ids.reshape(1, rows)
    return call(
        functools.partial(pack_kernel, dests=dests, groups=groups, kc=kc, fg=fg),
        (shape((dests * per_msg, LANES), bf16), shape((1, rows), jnp.int32)),
        (
            pltpu.VMEM((1, rows), jnp.int32),
            pltpu.VMEM((1, rows), jnp.int32),
            pltpu.VMEM((rows, width), bf16),
            pltpu.SemaphoreType.DMA((3,)),
            pltpu.VMEM((SLOTS * dests, rows), bf16),
            pltpu.VMEM((dests * per_msg, LANES), f32),
        ),
        in_specs=[pl.BlockSpec(memory_space=pltpu.HBM)] * 3,
    )(*(pltpu.with_memory_space_constraint(a, pltpu.HBM) for a in (ids[0], ids[1], embeddings)))


def update(msg, old, dests, groups, kc, fg):
    cells, width = old.shape
    slots, per_msg = SLOTS * dests, SLOTS * (width // LANES) + 2
    f32, bf16, shape = jnp.float32, jnp.bfloat16, jax.ShapeDtypeStruct
    return call(
        functools.partial(update_kernel, dests=dests, groups=groups, kc=kc, fg=fg),
        (
            shape((kc // 2, width + LANES), f32),
            shape((kc // 2, width + LANES), f32),
            shape((dests, SLOTS), f32),
            shape((cells, width), f32),
        ),
        (
            pltpu.VMEM((dests * per_msg, LANES), f32),
            pltpu.VMEM((slots, width), bf16),
            pltpu.VMEM((cells + kc, slots), bf16),
            pltpu.VMEM((cells, width), f32),
            pltpu.VMEM((cells * width // LANES, LANES), f32),
            pltpu.VMEM((cells, LANES), f32),
            pltpu.VMEM((dests, LANES), jnp.int32),
            pltpu.VMEM((dests // 16, LANES), jnp.int32),
            pltpu.SMEM((dests // 16, LANES), jnp.int32),
            pltpu.VMEM((slots, LANES), f32),
            pltpu.SemaphoreType.DMA((2,)),
        ),
        32 << 20,
        out_specs=(pl.BlockSpec(memory_space=pltpu.VMEM),) * 3 + (pl.BlockSpec(memory_space=pltpu.HBM),),
    )(msg, old)


def finish(back, pos, dests):
    return call(functools.partial(finish_kernel, dests=dests), jax.ShapeDtypeStruct(pos.shape, jnp.float32))(back, pos)


def on_device(embeddings, coarse_ids, fine_ids, coarse_old, fine_old):
    groups = lax.axis_size("grp")
    dests = lax.axis_size("rows") * groups
    rows, width = embeddings.shape
    kc, fg = fine_old.shape[:2]
    cells = kc * fg
    per_msg = SLOTS * (width // LANES) + 2
    msg, pos = pack(coarse_ids, fine_ids, embeddings, dests, groups, kc, fg)
    msg = lax.all_to_all(msg.reshape(dests, per_msg // 2, 2, LANES), AXES, 0, 0, tiled=True)
    coarse, away, dist, new = update(msg.reshape(-1, LANES), fine_old.reshape(cells, width), dests, groups, kc, fg)
    back = lax.all_to_all(dist, AXES, 0, 0, tiled=True)
    rounds = log2(groups)
    coarse = coarse + lax.ppermute(away, "grp", [(g, g ^ 1) for g in range(groups)])
    owned = kc // groups
    parts = [coarse[:owned]]
    for p in range(1, groups // 2):
        partner = sum(((p >> b) & 1) << (rounds - 1 - b) for b in range(rounds))
        parts.append(lax.ppermute(coarse[p * owned : (p + 1) * owned], "grp", [(g, g ^ partner) for g in range(groups)]))
    coarse = functools.reduce(jnp.add, parts)
    coarse_new = (coarse_old + coarse[:, :width]) / (1.0 + coarse[:, width : width + 1])
    distances = finish(back, pos, dests)
    return (coarse_new, new.reshape(fine_old.shape), distances.reshape(rows))


def solution(mesh):
    return jax.shard_map(
        on_device,
        mesh=mesh,
        in_specs=(
            P(AXES, None),
            P(AXES),
            P(AXES),
            P(AXES, None),
            P("rows", "grp", None),
        ),
        out_specs=(P(AXES, None), P("rows", "grp", None), P(AXES)),
        check_vma=False,
    )
```

time: 106 us -> 106 us (level)
  no operation moved by 1% of the time
where the time goes in v5:
time: 106 us; the launch traced here: 105 us
  blocking collectives  90.9 us (86%)
  Pallas kernels  7.4 us (7%)
  starting transfers between devices  4.59 us (4%)
    all_to_all x1, blocking collectives, on_device(): lax.all_to_all(msg.reshape(dests, per_msg // 2, 2, LANES), AXES, 0, 0, ti...  71.6 us
    all_to_all x1, blocking collectives, on_device(): back = lax.all_to_all(dist, AXES, 0, 0, tiled=True)  19.3 us
    pallas_call x1, Pallas kernels, update(): call(functools.partial(update_kernel, dests=dests, groups=groups, kc=kc,...  3.83 us
    ppermute x3, starting transfers between devices, on_device(): lax.ppermute(coarse[p * owned:(p + 1) * owned], 'grp', [(g, g ^ partner)...  3.73 us
    pallas_call x1, Pallas kernels, pack(): call(functools.partial(pack_kernel, dests=dests, groups=groups, kc=kc, fg...  2.7 us
  transfers between devices with their start and end apart: 4, of which 1 were waited for; matrix products, arithmetic and copies ran while one was open for 0% of the time, Pallas kernels for 1%

profile of v5, /device:TPU:1, one launch (start us, length us, event | category | flops | bytes accessed | tf_op | source)
XLA Modules:
  0.0 105.5 jit_solution(7201340995386977841)
XLA Ops:
  0.6 2.7 %shard_map.76 = (bf16[8704,128]{1,0:T(8,128)(2,1)S(1)}, s32[1,512]{1,0:T(1,128)S(1)}) custom-call(s32[1,512]{1,0:T(1,128)} %bitcast.16, s32[1,512]{1,0:T(1,128)} %bitcast.17, bf16[512,1024]{1,0:T(8,128)(2,1)} %emb_hbm.1), custom_call_target="tpu_custom_call" | custom-call | tf_op jit(solution)/shard_map/pallas_call | solution.py:232
  3.3 0.0 copy-start
  3.4 71.6 %all_to_all.16 = bf16[256,17,2,128]{3,2,1,0:T(2,128)(2,1)S(1)} all-to-all(bf16[256,17,2,128]{3,2,1,0:T(2,128)(2,1)S(1)} %bitcast.12), channel_id=1, replica_groups=mesh['rows'=32,'grp'=8] {'rows','grp'}, dimensions={0} | all-to-all | bytes 4456448 | tf_op jit(solution)/shard_map/all_to_all | solution.py:289
  75.0 0.0 copy-done
  75.0 0.0 copy-start.1
  75.0 3.8 %shard_map.77 = (f32[32,1152]{1,0:T(8,128)S(1)}, f32[32,1152]{1,0:T(8,128)S(1)}, f32[256,4]{1,0:T(8,128)S(1)}, f32[512,1024]{1,0:T(8,128)}) custom-call(bf16[8704,128]{1,0:T(8,128)(2,1)S(1)} %bitcast.11, f32[512,1024]{1,0:T(8,128)S(1)} %bitcast.13), custom_call_target="tpu_custom_call" | custom-call | tf_op jit(solution)/shard_map/pallas_call | solution.py:251
  78.8 0.9 collective-permute-start
  79.7 1.0 collective-permute-done
  80.7 2.6 %collective-permute-start.1 = (f32[8,1152]{1,0:T(8,128)S(1)}, f32[8,1152]{1,0:T(8,128)S(1)}, u32[]{:S(2)}, u32[]{:S(2)}) collective-permute-start(f32[8,1152]{1,0:T(8,128)S(1)} %get-tuple-element.15), channel_id=1, source_target_pairs={{0,4},{1,5},{2,6},{3,7},{4,0},{5,1},{6,2},{7,3},{8,12},{9,13},{10,... | collective-permute-start | bytes 110600 | tf_op jit(solution)/shard_map/ppermute | solution.py:298
  83.3 1.1 %collective-permute-start.3 = (f32[8,1152]{1,0:T(8,128)S(1)}, f32[8,1152]{1,0:T(8,128)S(1)}, u32[]{:S(2)}, u32[]{:S(2)}) collective-permute-start(f32[8,1152]{1,0:T(8,128)S(1)} %get-tuple-element.16), channel_id=1, source_target_pairs={{0,6},{1,7},{2,4},{3,5},{4,2},{5,3},{6,0},{7,1},{8,14},{9,15},{10,... | collective-permute-start | bytes 110600 | tf_op jit(solution)/shard_map/ppermute | solution.py:298
  84.5 0.0 collective-permute-start.2
  84.5 19.3 %all_to_all.17 = f32[256,1,4]{2,1,0:T(1,128)S(1)} all-to-all(f32[256,1,4]{2,1,0:T(1,128)S(1)} %bitcast.15), channel_id=1, replica_groups=mesh['rows'=32,'grp'=8] {'rows','grp'}, dimensions={0} | all-to-all | bytes 8192 | tf_op jit(solution)/shard_map/all_to_all | solution.py:291
  103.8 0.9 shard_map.78
  104.6 0.0 collective-permute-done.1
  104.6 0.0 collective-permute-done.3
  104.6 0.0 collective-permute-done.2
  104.7 0.1 fusion.3
  104.8 0.0 copy-done.1
  104.8 0.7 fusion.2
  (3 shorter events, 0.0 us)
Async XLA Ops:
  3.3 71.6 %copy-start = (f32[64,8,1024]{2,1,0:T(8,128)S(1)}, f32[64,8,1024]{2,1,0:T(8,128)}, u32[]{:S(2)}) copy-start(f32[64,8,1024]{2,1,0:T(8,128)} %param.9) | copy-start | bytes 6291460
  75.0 29.8 %copy-start.1 = (f32[8,1024]{1,0:T(8,128)S(1)}, f32[8,1024]{1,0:T(8,128)}, u32[]{:S(2)}) copy-start(f32[8,1024]{1,0:T(8,128)} %param.8) | copy-start | bytes 98308
  78.8 1.9 %collective-permute-start = (f32[32,1152]{1,0:T(8,128)S(1)}, f32[32,1152]{1,0:T(8,128)S(1)}, u32[]{:S(2)}, u32[]{:S(2)}) collective-permute-start(f32[32,1152]{1,0:T(8,128)S(1)} %get-tuple-element.11), channel_id=1, source_target_pairs={{0,1},{1,0},{2,3},{3,2},{4,5},{5,4},{6,7},{7,6},{8,9},{9,8},{10,11... | collective-permute-start | bytes 442376 | tf_op jit(solution)/shard_map/ppermute | solution.py:293
  80.7 23.9 %collective-permute-start.1 = (f32[8,1152]{1,0:T(8,128)S(1)}, f32[8,1152]{1,0:T(8,128)S(1)}, u32[]{:S(2)}, u32[]{:S(2)}) collective-permute-start(f32[8,1152]{1,0:T(8,128)S(1)} %get-tuple-element.15), channel_id=1, source_target_pairs={{0,4},{1,5},{2,6},{3,7},{4,0},{5,1},{6,2},{7,3},{8,12},{9,13},{10,... | collective-permute-start | bytes 110600 | tf_op jit(solution)/shard_map/ppermute | solution.py:298
  83.3 21.3 %collective-permute-start.3 = (f32[8,1152]{1,0:T(8,128)S(1)}, f32[8,1152]{1,0:T(8,128)S(1)}, u32[]{:S(2)}, u32[]{:S(2)}) collective-permute-start(f32[8,1152]{1,0:T(8,128)S(1)} %get-tuple-element.16), channel_id=1, source_target_pairs={{0,6},{1,7},{2,4},{3,5},{4,2},{5,3},{6,0},{7,1},{8,14},{9,15},{10,... | collective-permute-start | bytes 110600 | tf_op jit(solution)/shard_map/ppermute | solution.py:298
  84.5 20.2 %collective-permute-start.2 = (f32[8,1152]{1,0:T(8,128)S(1)}, f32[8,1152]{1,0:T(8,128)S(1)}, u32[]{:S(2)}, u32[]{:S(2)}) collective-permute-start(f32[8,1152]{1,0:T(8,128)S(1)} %get-tuple-element.17), channel_id=1, source_target_pairs={{0,2},{1,3},{2,0},{3,1},{4,6},{5,7},{6,4},{7,5},{8,10},{9,11},{10,... | collective-permute-start | bytes 110600 | tf_op jit(solution)/shard_map/ppermute | solution.py:298

commit v6 on v5

--- a/solution.py
+++ b/solution.py
@@ -49,7 +49,6 @@
     rows, width = emb_ref.shape
     lane_groups = width // LANES
     per_msg = SLOTS * lane_groups + 2
-    part = dests
     coarse_copy.wait()
     fine_copy.wait()
     coarse, fine = coarse_ref[...], fine_ref[...]
@@ -66,32 +65,27 @@
     half = LANES // 2
     names = jnp.where(iota((LANES, rows), 0) < half, (coarse & (kc - 1)) + 1, fine & (fg - 1))
     names = jnp.transpose(names.astype(jnp.float32)).astype(jnp.bfloat16)
-    lane = iota((part, LANES), 1)
+    lane = iota((dests, LANES), 1)
+    for s in range(SLOTS):
+        hit = iota((dests, rows), 0) + s * dests == pos
+        hot_ref[s * dests : (s + 1) * dests, :] = jnp.where(hit, 1.0, 0.0).astype(jnp.bfloat16)
+    got = jnp.dot(hot_ref[...], names, preferred_element_type=jnp.float32)
+    named = jnp.zeros((dests, LANES), jnp.float32)
+    for s in range(SLOTS):
+        named = jnp.where(lane & (half - 1) == s, got[s * dests : (s + 1) * dests], named)
+    at = SLOTS * lane_groups
+    wide_ref[pl.ds(at, dests, stride=per_msg), :] = named - jnp.where(lane < half, 1.0, 0.0)
+    wide_ref[pl.ds(at + 1, dests, stride=per_msg), :] = jnp.zeros((dests, LANES), jnp.float32)
+    emb_copy.wait()
     step = 2 * LANES
-    for p in range(0, dests, part):
-        for s in range(SLOTS):
-            hit = iota((part, rows), 0) + (s * dests + p) == pos
-            hot_ref[p * SLOTS + s * part : p * SLOTS + (s + 1) * part, :] = jnp.where(hit, 1.0, 0.0).astype(jnp.bfloat16)
-    for p in range(0, dests, part):
-        hot = hot_ref[p * SLOTS : (p + part) * SLOTS, :]
-        got = jnp.dot(hot, names, preferred_element_type=jnp.float32)
-        named = jnp.zeros((part, LANES), jnp.float32)
-        for s in range(SLOTS):
-            named = jnp.where(lane & (half - 1) == s, got[s * part : (s + 1) * part], named)
-        at = p * per_msg + SLOTS * lane_groups
-        wide_ref[pl.ds(at, part, stride=per_msg), :] = named - jnp.where(lane < half, 1.0, 0.0)
-        wide_ref[pl.ds(at + 1, part, stride=per_msg), :] = jnp.zeros((part, LANES), jnp.float32)
-    emb_copy.wait()
-    for p in range(0, dests, part):
-        hot = hot_ref[p * SLOTS : (p + part) * SLOTS, :]
-        for n in range(width // step):
-            got = jnp.dot(hot, emb_ref[:, n * step : (n + 1) * step], preferred_element_type=jnp.float32)
-            for h in range(2):
-                for s in range(SLOTS):
-                    at = p * per_msg + s * lane_groups + 2 * n + h
-                    wide_ref[pl.ds(at, part, stride=per_msg), :] = got[s * part : (s + 1) * part, h * LANES : (h + 1) * LANES]
-        at = slice(p * per_msg, (p + part) * per_msg)
-        msg_ref[at, :] = wide_ref[at, :].astype(jnp.bfloat16)
+    for n in range(width // step):
+        got = jnp.dot(hot_ref[...], emb_ref[:, n * step : (n + 1) * step], preferred_element_type=jnp.float32)
+        for h in range(2):
+            for s in range(SLOTS):
+                wide_ref[pl.ds(s * lane_groups + 2 * n + h, dests, stride=per_msg), :] = got[
+                    s * dests : (s + 1) * dests, h * LANES : (h + 1) * LANES
+                ]
+    msg_ref[...] = wide_ref[...].astype(jnp.bfloat16)
 
 
 def fold(parts):
@@ -118,7 +112,6 @@
     dist_ref,
     out_hbm,
     wide_ref,
-    x_ref,
     mem_ref,
     new_ref,
     tall_ref,
@@ -155,10 +148,6 @@
     key_copy.start()
     across = jnp.transpose(key)[:8].astype(jnp.int32)
     keys = jnp.concatenate([across[s : s + 1, :] for s in range(SLOTS)], axis=1)
-    for s in range(SLOTS):
-        for g in range(lane_groups):
-            part = wide_ref[pl.ds(s * lane_groups + g, dests, stride=per_msg), :]
-            x_ref[s * dests : (s + 1) * dests, g * LANES : (g + 1) * LANES] = part.astype(jnp.bfloat16)
     member = jnp.where(iota((cells, slots), 0) == keys, 1.0, 0.0)
     mem_ref[:cells, :] = member.astype(jnp.bfloat16)
     block = iota((kc, slots), 0) >> log2(kc // groups)
@@ -172,18 +161,32 @@
     send_ref[:, width:] = counts[cells + kc // 2 :]
     share_ref[...] = 1.0 / (1.0 + counts[:cells])
     step = 2 * LANES
+    out_copies = []
     for n in range(width // step):
         at = slice(n * step, (n + 1) * step)
-        sums = jnp.dot(mem_ref[...], x_ref[:, at], preferred_element_type=jnp.float32)
+        x = jnp.concatenate(
+            [
+                jnp.concatenate(
+                    [
+                        wide_ref[pl.ds(s * lane_groups + 2 * n + h, dests, stride=per_msg), :].astype(jnp.bfloat16)
+                        for h in range(2)
+                    ],
+                    axis=1,
+                )
+                for s in range(SLOTS)
+            ],
+            axis=0,
+        )
+        sums = jnp.dot(mem_ref[...], x, preferred_element_type=jnp.float32)
         for h in range(2):
             part = slice((2 * n + h) * LANES, (2 * n + h + 1) * LANES)
             new = (old_ref[:, part] + sums[:cells, h * LANES : (h + 1) * LANES]) * share_ref[...]
             new_ref[:, part] = new
             tall_ref[pl.ds(2 * n + h, cells, stride=lane_groups), :] = new
+        out_copies.append(pltpu.make_async_copy(new_ref.at[:, at], out_hbm.at[:, at], sems.at[1 + n]))
+        out_copies[n].start()
         keep_ref[:, at] = sums[cells : cells + kc // 2]
         send_ref[:, at] = sums[cells + kc // 2 :]
-    out_copy = pltpu.make_async_copy(new_ref, out_hbm, sems.at[1])
-    out_copy.start()
     key_copy.wait()
 
     for i in range(steps):
@@ -201,7 +204,8 @@
     for s in range(SLOTS):
         total = jnp.sum(gap_ref[s * dests : (s + 1) * dests, :], axis=1, keepdims=True)
         dist_ref[:, s : s + 1] = total * (1.0 / width)
-    out_copy.wait()
+    for copy in out_copies:
+        copy.wait()
 
 
 def finish_kernel(back_ref, pos_ref, out_ref, *, dests):
@@ -258,7 +262,6 @@
         ),
         (
             pltpu.VMEM((dests * per_msg, LANES), f32),
-            pltpu.VMEM((slots, width), bf16),
             pltpu.VMEM((cells + kc, slots), bf16),
             pltpu.VMEM((cells, width), f32),
             pltpu.VMEM((cells * width // LANES, LANES), f32),
@@ -267,7 +270,7 @@
             pltpu.VMEM((dests // 16, LANES), jnp.int32),
             pltpu.SMEM((dests // 16, LANES), jnp.int32),
             pltpu.VMEM((slots, LANES), f32),
-            pltpu.SemaphoreType.DMA((2,)),
+            pltpu.SemaphoreType.DMA((1 + width // (2 * LANES),)),
         ),
         32 << 20,
         out_specs=(pl.BlockSpec(memory_space=pltpu.VMEM),) * 3 + (pl.BlockSpec(memory_space=pltpu.HBM),),

time: 106 us -> 105 us (level)
  no operation moved by 1% of the time
where the time goes in v6:
time: 105 us
  blocking collectives  90.9 us (87%)
  Pallas kernels  6.91 us (7%)
  starting transfers between devices  4.57 us (4%)
    all_to_all x1, blocking collectives, on_device(): lax.all_to_all(msg.reshape(dests, per_msg // 2, 2, LANES), AXES, 0, 0, ti...  71.6 us
    all_to_all x1, blocking collectives, on_device(): back = lax.all_to_all(dist, AXES, 0, 0, tiled=True)  19.3 us
    ppermute x3, starting transfers between devices, on_device(): lax.ppermute(coarse[p * owned:(p + 1) * owned], 'grp', [(g, g ^ partner)...  3.71 us
    pallas_call x1, Pallas kernels, update(): call(functools.partial(update_kernel, dests=dests, groups=groups, kc=kc,...  3.34 us
    pallas_call x1, Pallas kernels, pack(): call(functools.partial(pack_kernel, dests=dests, groups=groups, kc=kc, fg...  2.7 us
  transfers between devices with their start and end apart: 4, of which 1 were waited for; matrix products, arithmetic and copies ran while one was open for 0% of the time, Pallas kernels for 1%

profile of v6, /device:TPU:1, one launch (start us, length us, event | category | flops | bytes accessed | tf_op | source)
XLA Modules:
  0.0 105.0 jit_solution(13506894553189545261)
XLA Ops:
  0.6 2.7 %shard_map.76 = (bf16[8704,128]{1,0:T(8,128)(2,1)S(1)}, s32[1,512]{1,0:T(1,128)S(1)}) custom-call(s32[1,512]{1,0:T(1,128)} %bitcast.16, s32[1,512]{1,0:T(1,128)} %bitcast.17, bf16[512,1024]{1,0:T(8,128)(2,1)} %emb_hbm.1), custom_call_target="tpu_custom_call" | custom-call | tf_op jit(solution)/shard_map/pallas_call | solution.py:236
  3.3 0.0 copy-start
  3.4 71.6 %all_to_all.16 = bf16[256,17,2,128]{3,2,1,0:T(2,128)(2,1)S(1)} all-to-all(bf16[256,17,2,128]{3,2,1,0:T(2,128)(2,1)S(1)} %bitcast.12), channel_id=1, replica_groups=mesh['rows'=32,'grp'=8] {'rows','grp'}, dimensions={0} | all-to-all | bytes 4456448 | tf_op jit(solution)/shard_map/all_to_all | solution.py:292
  75.0 0.0 copy-done
  75.0 0.0 copy-start.1
  75.0 3.3 %shard_map.77 = (f32[32,1152]{1,0:T(8,128)S(1)}, f32[32,1152]{1,0:T(8,128)S(1)}, f32[256,4]{1,0:T(8,128)S(1)}, f32[512,1024]{1,0:T(8,128)}) custom-call(bf16[8704,128]{1,0:T(8,128)(2,1)S(1)} %bitcast.11, f32[512,1024]{1,0:T(8,128)S(1)} %bitcast.13), custom_call_target="tpu_custom_call" | custom-call | tf_op jit(solution)/shard_map/pallas_call | solution.py:255
  78.3 0.9 collective-permute-start
  79.2 1.0 collective-permute-done
  80.2 2.6 %collective-permute-start.1 = (f32[8,1152]{1,0:T(8,128)S(1)}, f32[8,1152]{1,0:T(8,128)S(1)}, u32[]{:S(2)}, u32[]{:S(2)}) collective-permute-start(f32[8,1152]{1,0:T(8,128)S(1)} %get-tuple-element.15), channel_id=1, source_target_pairs={{0,4},{1,5},{2,6},{3,7},{4,0},{5,1},{6,2},{7,3},{8,12},{9,13},{10,... | collective-permute-start | bytes 110600 | tf_op jit(solution)/shard_map/ppermute | solution.py:301
  82.8 1.1 %collective-permute-start.3 = (f32[8,1152]{1,0:T(8,128)S(1)}, f32[8,1152]{1,0:T(8,128)S(1)}, u32[]{:S(2)}, u32[]{:S(2)}) collective-permute-start(f32[8,1152]{1,0:T(8,128)S(1)} %get-tuple-element.16), channel_id=1, source_target_pairs={{0,6},{1,7},{2,4},{3,5},{4,2},{5,3},{6,0},{7,1},{8,14},{9,15},{10,... | collective-permute-start | bytes 110600 | tf_op jit(solution)/shard_map/ppermute | solution.py:301
  83.9 0.0 collective-permute-start.2
  83.9 19.3 %all_to_all.17 = f32[256,1,4]{2,1,0:T(1,128)S(1)} all-to-all(f32[256,1,4]{2,1,0:T(1,128)S(1)} %bitcast.15), channel_id=1, replica_groups=mesh['rows'=32,'grp'=8] {'rows','grp'}, dimensions={0} | all-to-all | bytes 8192 | tf_op jit(solution)/shard_map/all_to_all | solution.py:294
  103.3 0.9 shard_map.78
  104.1 0.0 collective-permute-done.1
  104.1 0.0 collective-permute-done.3
  104.1 0.0 collective-permute-done.2
  104.2 0.1 fusion.3
  104.3 0.0 copy-done.1
  104.3 0.7 fusion.2
  (3 shorter events, 0.0 us)
Async XLA Ops:
  3.3 71.6 %copy-start = (f32[64,8,1024]{2,1,0:T(8,128)S(1)}, f32[64,8,1024]{2,1,0:T(8,128)}, u32[]{:S(2)}) copy-start(f32[64,8,1024]{2,1,0:T(8,128)} %param.9) | copy-start | bytes 6291460
  75.0 29.3 %copy-start.1 = (f32[8,1024]{1,0:T(8,128)S(1)}, f32[8,1024]{1,0:T(8,128)}, u32[]{:S(2)}) copy-start(f32[8,1024]{1,0:T(8,128)} %param.8) | copy-start | bytes 98308
  78.3 1.9 %collective-permute-start = (f32[32,1152]{1,0:T(8,128)S(1)}, f32[32,1152]{1,0:T(8,128)S(1)}, u32[]{:S(2)}, u32[]{:S(2)}) collective-permute-start(f32[32,1152]{1,0:T(8,128)S(1)} %get-tuple-element.11), channel_id=1, source_target_pairs={{0,1},{1,0},{2,3},{3,2},{4,5},{5,4},{6,7},{7,6},{8,9},{9,8},{10,11... | collective-permute-start | bytes 442376 | tf_op jit(solution)/shard_map/ppermute | solution.py:296
  80.2 23.9 %collective-permute-start.1 = (f32[8,1152]{1,0:T(8,128)S(1)}, f32[8,1152]{1,0:T(8,128)S(1)}, u32[]{:S(2)}, u32[]{:S(2)}) collective-permute-start(f32[8,1152]{1,0:T(8,128)S(1)} %get-tuple-element.15), channel_id=1, source_target_pairs={{0,4},{1,5},{2,6},{3,7},{4,0},{5,1},{6,2},{7,3},{8,12},{9,13},{10,... | collective-permute-start | bytes 110600 | tf_op jit(solution)/shard_map/ppermute | solution.py:301
  82.8 21.3 %collective-permute-start.3 = (f32[8,1152]{1,0:T(8,128)S(1)}, f32[8,1152]{1,0:T(8,128)S(1)}, u32[]{:S(2)}, u32[]{:S(2)}) collective-permute-start(f32[8,1152]{1,0:T(8,128)S(1)} %get-tuple-element.16), channel_id=1, source_target_pairs={{0,6},{1,7},{2,4},{3,5},{4,2},{5,3},{6,0},{7,1},{8,14},{9,15},{10,... | collective-permute-start | bytes 110600 | tf_op jit(solution)/shard_map/ppermute | solution.py:301
  83.9 20.2 %collective-permute-start.2 = (f32[8,1152]{1,0:T(8,128)S(1)}, f32[8,1152]{1,0:T(8,128)S(1)}, u32[]{:S(2)}, u32[]{:S(2)}) collective-permute-start(f32[8,1152]{1,0:T(8,128)S(1)} %get-tuple-element.17), channel_id=1, source_target_pairs={{0,2},{1,3},{2,0},{3,1},{4,6},{5,7},{6,4},{7,5},{8,10},{9,11},{10,... | collective-permute-start | bytes 110600 | tf_op jit(solution)/shard_map/ppermute | solution.py:301

commit v7 on v6

--- a/solution.py
+++ b/solution.py
@@ -77,12 +77,12 @@
     wide_ref[pl.ds(at, dests, stride=per_msg), :] = named - jnp.where(lane < half, 1.0, 0.0)
     wide_ref[pl.ds(at + 1, dests, stride=per_msg), :] = jnp.zeros((dests, LANES), jnp.float32)
     emb_copy.wait()
-    step = 2 * LANES
+    step = 8 * LANES
     for n in range(width // step):
         got = jnp.dot(hot_ref[...], emb_ref[:, n * step : (n + 1) * step], preferred_element_type=jnp.float32)
-        for h in range(2):
+        for h in range(8):
             for s in range(SLOTS):
-                wide_ref[pl.ds(s * lane_groups + 2 * n + h, dests, stride=per_msg), :] = got[
+                wide_ref[pl.ds(s * lane_groups + 8 * n + h, dests, stride=per_msg), :] = got[
                     s * dests : (s + 1) * dests, h * LANES : (h + 1) * LANES
                 ]
     msg_ref[...] = wide_ref[...].astype(jnp.bfloat16)
@@ -160,7 +160,7 @@
     keep_ref[:, width:] = counts[cells : cells + kc // 2]
     send_ref[:, width:] = counts[cells + kc // 2 :]
     share_ref[...] = 1.0 / (1.0 + counts[:cells])
-    step = 2 * LANES
+    step = 4 * LANES
     out_copies = []
     for n in range(width // step):
         at = slice(n * step, (n + 1) * step)
@@ -168,8 +168,8 @@
             [
                 jnp.concatenate(
                     [
-                        wide_ref[pl.ds(s * lane_groups + 2 * n + h, dests, stride=per_msg), :].astype(jnp.bfloat16)
-                        for h in range(2)
+                        wide_ref[pl.ds(s * lane_groups + 4 * n + h, dests, stride=per_msg), :].astype(jnp.bfloat16)
+                        for h in range(4)
                     ],
                     axis=1,
                 )
@@ -178,11 +178,11 @@
             axis=0,
         )
         sums = jnp.dot(mem_ref[...], x, preferred_element_type=jnp.float32)
-        for h in range(2):
-            part = slice((2 * n + h) * LANES, (2 * n + h + 1) * LANES)
+        for h in range(4):
+            part = slice((4 * n + h) * LANES, (4 * n + h + 1) * LANES)
             new = (old_ref[:, part] + sums[:cells, h * LANES : (h + 1) * LANES]) * share_ref[...]
             new_ref[:, part] = new
-            tall_ref[pl.ds(2 * n + h, cells, stride=lane_groups), :] = new
+            tall_ref[pl.ds(4 * n + h, cells, stride=lane_groups), :] = new
         out_copies.append(pltpu.make_async_copy(new_ref.at[:, at], out_hbm.at[:, at], sems.at[1 + n]))
         out_copies[n].start()
         keep_ref[:, at] = sums[cells : cells + kc // 2]
@@ -270,7 +270,7 @@
             pltpu.VMEM((dests // 16, LANES), jnp.int32),
             pltpu.SMEM((dests // 16, LANES), jnp.int32),
             pltpu.VMEM((slots, LANES), f32),
-            pltpu.SemaphoreType.DMA((1 + width // (2 * LANES),)),
+            pltpu.SemaphoreType.DMA((1 + width // (4 * LANES),)),
         ),
         32 << 20,
         out_specs=(pl.BlockSpec(memory_space=pltpu.VMEM),) * 3 + (pl.BlockSpec(memory_space=pltpu.HBM),),

time: 105 us -> 105 us (level)
  no operation moved by 1% of the time
where the time goes in v7:
time: 105 us
  blocking collectives  90.9 us (87%)
  Pallas kernels  6.76 us (6%)
  starting transfers between devices  4.59 us (4%)
    all_to_all x1, blocking collectives, on_device(): lax.all_to_all(msg.reshape(dests, per_msg // 2, 2, LANES), AXES, 0, 0, ti...  71.6 us
    all_to_all x1, blocking collectives, on_device(): back = lax.all_to_all(dist, AXES, 0, 0, tiled=True)  19.3 us
    ppermute x3, starting transfers between devices, on_device(): lax.ppermute(coarse[p * owned:(p + 1) * owned], 'grp', [(g, g ^ partner)...  3.73 us
    pallas_call x1, Pallas kernels, update(): call(functools.partial(update_kernel, dests=dests, groups=groups, kc=kc,...  3.19 us
    pallas_call x1, Pallas kernels, pack(): call(functools.partial(pack_kernel, dests=dests, groups=groups, kc=kc, fg...  2.7 us
  transfers between devices with their start and end apart: 4, of which 1 were waited for; matrix products, arithmetic and copies ran while one was open for 0% of the time, Pallas kernels for 1%

profile of v7, /device:TPU:1, one launch (start us, length us, event | category | flops | bytes accessed | tf_op | source)
XLA Modules:
  0.0 104.8 jit_solution(8819419103183934244)
XLA Ops:
  0.6 2.7 %shard_map.76 = (bf16[8704,128]{1,0:T(8,128)(2,1)S(1)}, s32[1,512]{1,0:T(1,128)S(1)}) custom-call(s32[1,512]{1,0:T(1,128)} %bitcast.16, s32[1,512]{1,0:T(1,128)} %bitcast.17, bf16[512,1024]{1,0:T(8,128)(2,1)} %emb_hbm.1), custom_call_target="tpu_custom_call" | custom-call | tf_op jit(solution)/shard_map/pallas_call | solution.py:236
  3.3 0.0 copy-start
  3.4 71.6 %all_to_all.16 = bf16[256,17,2,128]{3,2,1,0:T(2,128)(2,1)S(1)} all-to-all(bf16[256,17,2,128]{3,2,1,0:T(2,128)(2,1)S(1)} %bitcast.12), channel_id=1, replica_groups=mesh['rows'=32,'grp'=8] {'rows','grp'}, dimensions={0} | all-to-all | bytes 4456448 | tf_op jit(solution)/shard_map/all_to_all | solution.py:292
  75.0 0.0 copy-done
  75.0 0.0 copy-start.1
  75.0 3.2 %shard_map.77 = (f32[32,1152]{1,0:T(8,128)S(1)}, f32[32,1152]{1,0:T(8,128)S(1)}, f32[256,4]{1,0:T(8,128)S(1)}, f32[512,1024]{1,0:T(8,128)}) custom-call(bf16[8704,128]{1,0:T(8,128)(2,1)S(1)} %bitcast.11, f32[512,1024]{1,0:T(8,128)S(1)} %bitcast.13), custom_call_target="tpu_custom_call" | custom-call | tf_op jit(solution)/shard_map/pallas_call | solution.py:255
  78.2 0.9 collective-permute-start
  79.0 1.0 collective-permute-done
  80.1 2.6 %collective-permute-start.1 = (f32[8,1152]{1,0:T(8,128)S(1)}, f32[8,1152]{1,0:T(8,128)S(1)}, u32[]{:S(2)}, u32[]{:S(2)}) collective-permute-start(f32[8,1152]{1,0:T(8,128)S(1)} %get-tuple-element.15), channel_id=1, source_target_pairs={{0,4},{1,5},{2,6},{3,7},{4,0},{5,1},{6,2},{7,3},{8,12},{9,13},{10,... | collective-permute-start | bytes 110600 | tf_op jit(solution)/shard_map/ppermute | solution.py:301
  82.7 1.2 %collective-permute-start.3 = (f32[8,1152]{1,0:T(8,128)S(1)}, f32[8,1152]{1,0:T(8,128)S(1)}, u32[]{:S(2)}, u32[]{:S(2)}) collective-permute-start(f32[8,1152]{1,0:T(8,128)S(1)} %get-tuple-element.16), channel_id=1, source_target_pairs={{0,6},{1,7},{2,4},{3,5},{4,2},{5,3},{6,0},{7,1},{8,14},{9,15},{10,... | collective-permute-start | bytes 110600 | tf_op jit(solution)/shard_map/ppermute | solution.py:301
  83.8 0.0 collective-permute-start.2
  83.8 19.3 %all_to_all.17 = f32[256,1,4]{2,1,0:T(1,128)S(1)} all-to-all(f32[256,1,4]{2,1,0:T(1,128)S(1)} %bitcast.15), channel_id=1, replica_groups=mesh['rows'=32,'grp'=8] {'rows','grp'}, dimensions={0} | all-to-all | bytes 8192 | tf_op jit(solution)/shard_map/all_to_all | solution.py:294
  103.1 0.9 shard_map.78
  104.0 0.0 collective-permute-done.1
  104.0 0.0 collective-permute-done.3
  104.0 0.0 collective-permute-done.2
  104.0 0.1 fusion.3
  104.1 0.0 copy-done.1
  104.1 0.7 fusion.2
  (3 shorter events, 0.0 us)
Async XLA Ops:
  3.3 71.6 %copy-start = (f32[64,8,1024]{2,1,0:T(8,128)S(1)}, f32[64,8,1024]{2,1,0:T(8,128)}, u32[]{:S(2)}) copy-start(f32[64,8,1024]{2,1,0:T(8,128)} %param.9) | copy-start | bytes 6291460
  75.0 29.2 %copy-start.1 = (f32[8,1024]{1,0:T(8,128)S(1)}, f32[8,1024]{1,0:T(8,128)}, u32[]{:S(2)}) copy-start(f32[8,1024]{1,0:T(8,128)} %param.8) | copy-start | bytes 98308
  78.2 1.9 %collective-permute-start = (f32[32,1152]{1,0:T(8,128)S(1)}, f32[32,1152]{1,0:T(8,128)S(1)}, u32[]{:S(2)}, u32[]{:S(2)}) collective-permute-start(f32[32,1152]{1,0:T(8,128)S(1)} %get-tuple-element.11), channel_id=1, source_target_pairs={{0,1},{1,0},{2,3},{3,2},{4,5},{5,4},{6,7},{7,6},{8,9},{9,8},{10,11... | collective-permute-start | bytes 442376 | tf_op jit(solution)/shard_map/ppermute | solution.py:296
  80.1 23.9 %collective-permute-start.1 = (f32[8,1152]{1,0:T(8,128)S(1)}, f32[8,1152]{1,0:T(8,128)S(1)}, u32[]{:S(2)}, u32[]{:S(2)}) collective-permute-start(f32[8,1152]{1,0:T(8,128)S(1)} %get-tuple-element.15), channel_id=1, source_target_pairs={{0,4},{1,5},{2,6},{3,7},{4,0},{5,1},{6,2},{7,3},{8,12},{9,13},{10,... | collective-permute-start | bytes 110600 | tf_op jit(solution)/shard_map/ppermute | solution.py:301
  82.7 21.3 %collective-permute-start.3 = (f32[8,1152]{1,0:T(8,128)S(1)}, f32[8,1152]{1,0:T(8,128)S(1)}, u32[]{:S(2)}, u32[]{:S(2)}) collective-permute-start(f32[8,1152]{1,0:T(8,128)S(1)} %get-tuple-element.16), channel_id=1, source_target_pairs={{0,6},{1,7},{2,4},{3,5},{4,2},{5,3},{6,0},{7,1},{8,14},{9,15},{10,... | collective-permute-start | bytes 110600 | tf_op jit(solution)/shard_map/ppermute | solution.py:301
  83.8 20.2 %collective-permute-start.2 = (f32[8,1152]{1,0:T(8,128)S(1)}, f32[8,1152]{1,0:T(8,128)S(1)}, u32[]{:S(2)}, u32[]{:S(2)}) collective-permute-start(f32[8,1152]{1,0:T(8,128)S(1)} %get-tuple-element.17), channel_id=1, source_target_pairs={{0,2},{1,3},{2,0},{3,1},{4,6},{5,7},{6,4},{7,5},{8,10},{9,11},{10,... | collective-permute-start | bytes 110600 | tf_op jit(solution)/shard_map/ppermute | solution.py:301
